TPU v7x, 512 devices: a whole 4x4x16 slice. The times are simulated.
512 devices in a mesh: grp: 8 (over x, core), dev: 64 (over y, z).
Axes of the slice: x: 4, y: 4, z: 16, core: 2. Of those that a mesh axis runs over, the one named last changes fastest.
Arguments:
- line_bin: int32 [1048576], P(('grp', 'dev')), may hold values from 0 to 65535, as said below
- line_slot: int32 [1048576], P(('grp', 'dev')), may hold values from 0 to 31
- strength: float32 [1048576], P(('grp', 'dev')), may hold values from 0.05 to 1
- line_count: int32 [512], P(('grp', 'dev')), may hold values from 1024 to 2048
- gauss_width: float32 [32], replicated, may hold values from 2 to 40
- lorentz_width: float32 [32], replicated, may hold values from 1 to 30
- mixing: float32 [32], replicated, may hold values from 0.1 to 0.9
- profile_factor: float32 [32, 257], replicated, may hold values from 0.25 to 1.75
Outputs:
- spectrum: float32 [524288], P(('grp', 'dev'))
Inputs may be any that keep to these rules, and one draw needn't show every extreme that they name: `line_bin`: every line of device (g, d) (the d-th block of 2048 lines within the g-th group of 64 blocks) has a bin within (d - 2) * 1024 to (d + 3) * 1024 - 1 of its super-band.
All inputs are finite; a program needn't handle non-finite values.
Results may differ from a plain program's by a relative error of at most 0.00005.
Values sent between devices are 32-bit elements; how exact they have to be, the bound alone decides.
A program may use at most 64 MiB of HBM per device.

v0:
```python
import jax
import jax.numpy as jnp
from jax import lax
from jax.sharding import PartitionSpec as P

SLOTS = 32
WING = 128
HOP = 2
SPAN = 1024


def shifted(value, axis, by):
    devices = lax.axis_size(axis)
    pairs = [(i, i + by) for i in range(devices) if 0 <= i + by < devices]
    return lax.ppermute(value, axis, pairs)


def padded_2(value, sides, width):
    for axis, dim in sides:
        devices, length = (lax.axis_size(axis), value.shape[dim])
        up = [(i, (i + 1) % devices) for i in range(devices - 1)]
        down = [(j, i) for i, j in up]
        last = lax.slice_in_dim(value, length - width, length, axis=dim)
        first = lax.slice_in_dim(value, 0, width, axis=dim)
        before = lax.ppermute(last, axis, up)
        after = lax.ppermute(first, axis, down)
        value = jnp.concatenate([before, value, after], axis=dim)
    return value


def build_kernel(gauss_width, lorentz_width, mixing, profile_factor):
    offset = jnp.arange(-WING, WING + 1).astype(jnp.float32)
    square = offset[None, :] * offset[None, :]
    lorentz = (
        lorentz_width[:, None]
        * lorentz_width[:, None]
        / (square + lorentz_width[:, None] * lorentz_width[:, None])
    )
    gauss = jnp.exp(-square / (2.0 * gauss_width[:, None] * gauss_width[:, None]))
    raw = (mixing[:, None] * lorentz + (1.0 - mixing[:, None]) * gauss) * profile_factor
    return raw / jnp.sum(raw, axis=1, keepdims=True)


def convolve_padded(padded, kernel):
    spread = lax.conv_general_dilated(
        padded[None],
        kernel[:, None, :],
        (1,),
        [(0, 0)],
        feature_group_count=SLOTS,
        precision=lax.Precision.HIGHEST,
    )
    return jnp.sum(spread[0], axis=0)


def body(
    line_bin, line_slot, strength, line_count, gauss_width, lorentz_width, mixing, profile_factor
):
    lines = line_bin.shape[0]
    span_cells = SPAN
    reach = 2 * HOP + 1
    width = reach * span_cells
    anchor = (lax.axis_index("dev") - HOP) * span_cells
    live = jnp.arange(lines) < line_count[0]
    weight = jnp.where(live, strength, jnp.float32(0.0))
    flat = line_slot * width + (line_bin - anchor)
    grid = jnp.zeros((SLOTS * width,), jnp.float32).at[flat].add(weight).reshape(SLOTS, width)
    kernel = build_kernel(gauss_width, lorentz_width, mixing, profile_factor)
    blocks = grid.reshape(SLOTS, reach, span_cells)
    owned = blocks[:, HOP]
    for offset in [step for hop in range(1, HOP + 1) for step in (hop, -hop)]:
        owned = owned + shifted(blocks[:, HOP + offset], "dev", offset)
    padded = padded_2(owned, ((("grp", "dev"), 1),), WING)
    return convolve_padded(padded, kernel)


def solution(mesh):
    in_specs = (
        P(("grp", "dev")),
        P(("grp", "dev")),
        P(("grp", "dev")),
        P(("grp", "dev")),
        P(),
        P(),
        P(),
        P(),
    )
    out_specs = P(("grp", "dev"))
    return jax.shard_map(body, mesh=mesh, in_specs=in_specs, out_specs=out_specs, check_vma=False)
```

profile of v0, /device:TPU:24, one launch (start us, length us, event | category | flops | bytes accessed | tf_op | source)
XLA Modules:
  0.0 82.0 jit_solution(8202399885543795052)
XLA Ops:
  0.7 0.0 copy-done.3
  0.7 0.7 copy-done.1
  1.4 0.0 copy-done.2
  1.4 11.4 %scatter_custom_fusion = f32[163840]{0:T(1024)S(1)} fusion(s32[2048]{0:T(1024)S(1)} %compare_select_fusion, f32[2048]{0:T(1024)S(1)} %fusion.9, f32[]{:T(128)} %constant.10.clone.1), kind=kCustom, calls=%fused_computation.2 | custom fusion | flops 2048 | bytes 655364 | tf_op jit(solution)/shard_map/scatter-add | solution.py:67
  12.8 0.1 reshape_reshape.3
  12.9 0.5 fusion.13
  13.5 3.8 %collective-permute-start = (f32[32,1024]{1,0:T(8,128)S(1)}, f32[32,1024]{1,0:T(8,128)S(1)}, u32[]{:S(2)}, u32[]{:S(2)}) collective-permute-start(f32[32,1024]{1,0:T(8,128)S(1)} %bitcast.30), channel_id=1, source_target_pairs={{0,1},{1,2},{2,3},{3,4},{4,5},{5,6},{6,7},{7,8},{8,9},{9,10},{10,1... | collective-permute-start | bytes 393224 | tf_op jit(solution)/shard_map/ppermute | solution.py:15
  17.3 9.7 %collective-permute-start.1 = (f32[32,1024]{1,0:T(8,128)S(1)}, f32[32,1024]{1,0:T(8,128)S(1)}, u32[]{:S(2)}, u32[]{:S(2)}) collective-permute-start(f32[32,1024]{1,0:T(8,128)S(1)} %bitcast.31), channel_id=1, source_target_pairs={{1,0},{2,1},{3,2},{4,3},{5,4},{6,5},{7,6},{8,7},{9,8},{10,9},{11,1... | collective-permute-start | bytes 393224 | tf_op jit(solution)/shard_map/ppermute | solution.py:15
  27.1 1.9 %collective-permute-start.2 = (f32[32,1024]{1,0:T(8,128)S(1)}, f32[32,1024]{1,0:T(8,128)S(1)}, u32[]{:S(2)}, u32[]{:S(2)}) collective-permute-start(f32[32,1024]{1,0:T(8,128)S(1)} %bitcast.32), channel_id=1, source_target_pairs={{0,2},{1,3},{2,4},{3,5},{4,6},{5,7},{6,8},{7,9},{8,10},{9,11},{10,... | collective-permute-start | bytes 393224 | tf_op jit(solution)/shard_map/ppermute | solution.py:15
  29.0 0.0 copy-start
  29.0 0.0 copy-start.6
  29.0 6.9 %collective-permute-start.3 = (f32[32,1024]{1,0:T(8,128)S(1)}, f32[32,1024]{1,0:T(8,128)S(1)}, u32[]{:S(2)}, u32[]{:S(2)}) collective-permute-start(f32[32,1024]{1,0:T(8,128)S(1)} %bitcast.33), channel_id=1, source_target_pairs={{2,0},{3,1},{4,2},{5,3},{6,4},{7,5},{8,6},{9,7},{10,8},{11,9},{12,... | collective-permute-start | bytes 393224 | tf_op jit(solution)/shard_map/ppermute | solution.py:15
  36.0 0.0 copy-done.6
  36.0 0.0 copy-start.4
  36.0 0.0 copy-start.5
  36.0 0.6 copy-done.4
  36.7 0.0 copy-done.5
  36.7 0.0 copy-done
  36.7 0.2 fusion.11
  36.9 0.0 collective-permute-done
  36.9 0.0 collective-permute-done.1
  36.9 2.2 %collective-permute-done.2 = f32[32,1024]{1,0:T(8,128)S(1)} collective-permute-done((f32[32,1024]{1,0:T(8,128)S(1)}, f32[32,1024]{1,0:T(8,128)S(1)}, u32[]{:S(2)}, u32[]{:S(2)}) %collective-permute-start.2) | collective-permute-done | bytes 131104 | tf_op jit(solution)/shard_map/ppermute | solution.py:15
  39.1 0.9 %collective-permute-done.3 = f32[32,1024]{1,0:T(8,128)S(1)} collective-permute-done((f32[32,1024]{1,0:T(8,128)S(1)}, f32[32,1024]{1,0:T(8,128)S(1)}, u32[]{:S(2)}, u32[]{:S(2)}) %collective-permute-start.3) | collective-permute-done | bytes 131104 | tf_op jit(solution)/shard_map/ppermute | solution.py:15
  40.1 0.1 fusion.5
  40.2 1.9 %collective-permute-start.4 = (f32[32,128]{1,0:T(8,128)S(1)}, f32[32,128]{1,0:T(8,128)S(1)}, u32[]{:S(2)}, u32[]{:S(2)}) collective-permute-start(f32[32,128]{1,0:T(8,128)S(1)} %get-tuple-element.12), channel_id=1, source_target_pairs={{0,1},{1,2},{2,3},{3,4},{4,5},{5,6},{6,7},{7,8},{8,9},{9,10},{10,1... | collective-permute-start | bytes 49160 | tf_op jit(solution)/shard_map/ppermute | solution.py:25
  42.1 6.0 %collective-permute-start.5 = (f32[32,128]{1,0:T(8,128)S(1)}, f32[32,128]{1,0:T(8,128)S(1)}, u32[]{:S(2)}, u32[]{:S(2)}) collective-permute-start(f32[32,128]{1,0:T(8,128)S(1)} %get-tuple-element.13), channel_id=1, source_target_pairs={{1,0},{2,1},{3,2},{4,3},{5,4},{6,5},{7,6},{8,7},{9,8},{10,9},{11,1... | collective-permute-start | bytes 49160 | tf_op jit(solution)/shard_map/ppermute | solution.py:26
  48.1 0.1 divide_bitcast_fusion
  48.2 0.1 copy.21
  48.3 0.0 collective-permute-done.4
  48.3 1.2 %collective-permute-done.5 = f32[32,128]{1,0:T(8,128)S(1)} collective-permute-done((f32[32,128]{1,0:T(8,128)S(1)}, f32[32,128]{1,0:T(8,128)S(1)}, u32[]{:S(2)}, u32[]{:S(2)}) %collective-permute-start.5) | collective-permute-done | bytes 16416 | tf_op jit(solution)/shard_map/ppermute | solution.py:26
  49.6 0.2 copy.20
  49.8 32.2 %convolution_reduce_fusion = f32[1024]{0:T(1024)} fusion(f32[1,32,1280]{1,0,2:T(1,128)S(1)} %bitcast.29, f32[32,1,257]{0,1,2:T(1,128)S(1)} %copy.21), kind=kOutput, calls=%fused_computation.1 | convolution fusion | flops 101088256 | bytes 200832 | tf_op jit(solution)/shard_map/conv_general_dilated | solution.py:45
  (14 shorter events, 0.2 us)
Async XLA Ops:
  0.0 0.7 copy-start.3
  0.7 0.7 copy-start.1
  0.7 0.7 copy-start.2
  13.5 23.4 %collective-permute-start = (f32[32,1024]{1,0:T(8,128)S(1)}, f32[32,1024]{1,0:T(8,128)S(1)}, u32[]{:S(2)}, u32[]{:S(2)}) collective-permute-start(f32[32,1024]{1,0:T(8,128)S(1)} %bitcast.30), channel_id=1, source_target_pairs={{0,1},{1,2},{2,3},{3,4},{4,5},{5,6},{6,7},{7,8},{8,9},{9,10},{10,1... | collective-permute-start | bytes 393224 | tf_op jit(solution)/shard_map/ppermute | solution.py:15
  17.3 19.6 %collective-permute-start.1 = (f32[32,1024]{1,0:T(8,128)S(1)}, f32[32,1024]{1,0:T(8,128)S(1)}, u32[]{:S(2)}, u32[]{:S(2)}) collective-permute-start(f32[32,1024]{1,0:T(8,128)S(1)} %bitcast.31), channel_id=1, source_target_pairs={{1,0},{2,1},{3,2},{4,3},{5,4},{6,5},{7,6},{8,7},{9,8},{10,9},{11,1... | collective-permute-start | bytes 393224 | tf_op jit(solution)/shard_map/ppermute | solution.py:15
  27.1 12.1 %collective-permute-start.2 = (f32[32,1024]{1,0:T(8,128)S(1)}, f32[32,1024]{1,0:T(8,128)S(1)}, u32[]{:S(2)}, u32[]{:S(2)}) collective-permute-start(f32[32,1024]{1,0:T(8,128)S(1)} %bitcast.32), channel_id=1, source_target_pairs={{0,2},{1,3},{2,4},{3,5},{4,6},{5,7},{6,8},{7,9},{8,10},{9,11},{10,... | collective-permute-start | bytes 393224 | tf_op jit(solution)/shard_map/ppermute | solution.py:15
  29.0 7.7 %copy-start = (f32[32,257]{1,0:T(8,128)S(1)}, f32[32,257]{1,0:T(8,128)}, u32[]{:S(2)}) copy-start(f32[32,257]{1,0:T(8,128)} %param.15) | copy-start | bytes 98692
  29.0 7.0 %copy-start.6 = (f32[32]{0:T(128)S(1)}, f32[32]{0:T(128)}, u32[]{:S(2)}) copy-start(f32[32]{0:T(128)} %param.13) | copy-start | bytes 388
  29.0 11.1 %collective-permute-start.3 = (f32[32,1024]{1,0:T(8,128)S(1)}, f32[32,1024]{1,0:T(8,128)S(1)}, u32[]{:S(2)}, u32[]{:S(2)}) collective-permute-start(f32[32,1024]{1,0:T(8,128)S(1)} %bitcast.33), channel_id=1, source_target_pairs={{2,0},{3,1},{4,2},{5,3},{6,4},{7,5},{8,6},{9,7},{10,8},{11,9},{12,... | collective-permute-start | bytes 393224 | tf_op jit(solution)/shard_map/ppermute | solution.py:15
  36.0 0.7 copy-start.4
  36.0 0.7 copy-start.5
  40.2 8.2 %collective-permute-start.4 = (f32[32,128]{1,0:T(8,128)S(1)}, f32[32,128]{1,0:T(8,128)S(1)}, u32[]{:S(2)}, u32[]{:S(2)}) collective-permute-start(f32[32,128]{1,0:T(8,128)S(1)} %get-tuple-element.12), channel_id=1, source_target_pairs={{0,1},{1,2},{2,3},{3,4},{4,5},{5,6},{6,7},{7,8},{8,9},{9,10},{10,1... | collective-permute-start | bytes 49160 | tf_op jit(solution)/shard_map/ppermute | solution.py:25
  42.1 7.5 %collective-permute-start.5 = (f32[32,128]{1,0:T(8,128)S(1)}, f32[32,128]{1,0:T(8,128)S(1)}, u32[]{:S(2)}, u32[]{:S(2)}) collective-permute-start(f32[32,128]{1,0:T(8,128)S(1)} %get-tuple-element.13), channel_id=1, source_target_pairs={{1,0},{2,1},{3,2},{4,3},{5,4},{6,5},{7,6},{8,7},{9,8},{10,9},{11,1... | collective-permute-start | bytes 49160 | tf_op jit(solution)/shard_map/ppermute | solution.py:26
where the time goes:
time: 82.4 us; the launch traced here: 82 us
  matrix products  32.2 us (39%)
  starting transfers between devices  30.3 us (37%)
  other arithmetic  11.8 us (14%)
  waiting for transfers between devices  4.41 us (5%)
  local copies, waits for them, and re-layouts  2.42 us (3%)
  between operations  0.89 us (1%)
    conv_general_dilated x1, matrix products, convolve_padded(): lax.conv_general_dilated(padded[None], kernel[:, None, :], (1,), [(0, 0)]...  32.2 us
    ppermute x4, starting transfers between devices, shifted(): return lax.ppermute(value, axis, pairs)  22.4 us
    scatter-add x1, other arithmetic, body(): jnp.zeros((SLOTS * width,), jnp.float32).at[flat].add(weight)  11.4 us
    ppermute x1, starting transfers between devices, padded_2(): after = lax.ppermute(first, axis, down)  6.03 us
    ppermute x4, waiting for transfers between devices, shifted(): return lax.ppermute(value, axis, pairs)  3.2 us
    ppermute x1, starting transfers between devices, padded_2(): before = lax.ppermute(last, axis, up)  1.92 us
  transfers between devices with their start and end apart: 6, of which 3 were waited for; matrix products, arithmetic and copies ran while one was open for 1% of the time, Pallas kernels for 0%

commit v1 on v0

v1 whole, which is shorter than its diff:
```python
import jax
import jax.numpy as jnp
from jax import lax
from jax.experimental import pallas as pl
from jax.experimental.pallas import tpu as pltpu
from jax.sharding import PartitionSpec as P

SLOTS = 32
WING = 128
HOP = 2
SPAN = 1024
LANES = 128
OFFSETS = (-3, 3, -2, 2, -1, 1)
BF16 = jnp.bfloat16
F32 = jnp.float32
ROWS = (2 * HOP + 1) * SPAN // LANES
PART = 32
QUARTERS = LANES // PART
HALF = SLOTS // 2
TALL = 2 * QUARTERS * ROWS
WIDE = PART * HALF
REACH = 3 * LANES


def split(value):
    high = value.astype(BF16)
    low = (value - high.astype(F32)).astype(BF16)
    return high, low


def column(row):
    i = lax.broadcasted_iota(jnp.int32, (SLOTS, SLOTS), 0)
    j = lax.broadcasted_iota(jnp.int32, (SLOTS, SLOTS), 1)
    spread = jnp.where(i == j, jnp.broadcast_to(row, (SLOTS, SLOTS)), 0.0)
    return jnp.sum(spread, axis=1, keepdims=True)


def voigt_table(gauss_ref, lorentz_ref, mixing_ref, factor_ref, padded):
    padded[...] = jnp.zeros((SLOTS, REACH), F32)
    padded[:, 0 : 2 * WING + 1] = factor_ref[...]
    back = LANES - 1 - lax.broadcasted_iota(jnp.int32, (SLOTS, LANES), 1)
    pieces = [
        jnp.take_along_axis(
            padded[:, c * LANES : (c + 1) * LANES], back, axis=1, mode="promise_in_bounds"
        )
        for c in (2, 1, 0)
    ]
    factor = jnp.concatenate(pieces, axis=1)
    m = lax.broadcasted_iota(jnp.int32, (SLOTS, REACH), 1)
    offset = (REACH - 1 - WING - m).astype(F32)
    square = offset * offset
    gauss_width = column(gauss_ref[...])
    lorentz_width = column(lorentz_ref[...])
    mixing = column(mixing_ref[...])
    wide = lorentz_width * lorentz_width
    lorentz = wide / (square + wide)
    gauss = jnp.exp(-square / (2.0 * gauss_width * gauss_width))
    raw = (mixing * lorentz + (1.0 - mixing) * gauss) * factor
    raw = jnp.where(m >= REACH - 1 - 2 * WING, raw, 0.0)
    return raw / jnp.sum(raw, axis=1, keepdims=True)


def kernel(
    n_grp,
    n_dev,
    bin_ref,
    slot_ref,
    strength_ref,
    count_ref,
    gauss_ref,
    lorentz_ref,
    mixing_ref,
    factor_ref,
    out_ref,
    padded,
    t_high,
    t_low,
    a_ref,
    b_ref,
    tiles,
    inbox,
    send_sem,
    recv_sem,
):
    devices = n_grp * n_dev
    dev = lax.axis_index("dev")
    me = lax.axis_index("grp") * n_dev + dev

    barrier = pltpu.get_barrier_semaphore()
    peers = jnp.int32(0)
    for o in OFFSETS:
        there = jnp.logical_and(me + o >= 0, me + o < devices)
        peers = peers + there.astype(jnp.int32)

        @pl.when(there)
        def _():
            pl.semaphore_signal(
                barrier,
                inc=1,
                device_id=((me + o) // n_dev, (me + o) % n_dev),
                device_id_type=pl.DeviceIdType.MESH,
            )

    table = voigt_table(gauss_ref, lorentz_ref, mixing_ref, factor_ref, padded)
    for r in range(PART):
        high, low = split(pltpu.roll(table, r + 2 * LANES + 1, 1))
        for h in range(2):
            t_high[h * WIDE + r * HALF : h * WIDE + (r + 1) * HALF, :] = high[
                h * HALF : (h + 1) * HALF
            ]
            t_low[h * WIDE + r * HALF : h * WIDE + (r + 1) * HALF, :] = low[
                h * HALF : (h + 1) * HALF
            ]

    lines = bin_ref.shape[0] * LANES
    near = bin_ref[...] - (dev - HOP) * SPAN
    slot = slot_ref[...]
    tall = ((slot // HALF) * QUARTERS + (near // PART) % QUARTERS) * ROWS + near // LANES
    wide = (near % PART) * HALF + slot % HALF
    place = lax.broadcasted_iota(jnp.int32, near.shape, 0) * LANES + lax.broadcasted_iota(
        jnp.int32, near.shape, 1
    )
    weight = jnp.where(place < count_ref[...], strength_ref[...], 0.0)
    weight_high = weight.astype(BF16).astype(F32)
    weight_low = weight - weight_high
    wide = jnp.transpose(wide)
    tall_at = lax.broadcasted_iota(jnp.int32, (TALL, LANES), 0)
    wide_at = lax.broadcasted_iota(jnp.int32, (LANES, WIDE), 1)
    for k in range(lines // LANES):
        cols = slice(k * LANES, (k + 1) * LANES)
        hit = tall_at == tall[k : k + 1, :]
        a_ref[0:TALL, cols] = jnp.where(hit, weight_high[k : k + 1, :], 0.0).astype(BF16)
        a_ref[TALL : 2 * TALL, cols] = jnp.where(hit, weight_low[k : k + 1, :], 0.0).astype(BF16)
        b_ref[cols, :] = jnp.where(wide_at == wide[:, k : k + 1], 1.0, 0.0).astype(BF16)
    both = jnp.dot(a_ref[...], b_ref[...], preferred_element_type=F32)
    grid = both[0:TALL] + both[TALL : 2 * TALL]

    rows = QUARTERS * ROWS
    total = jnp.zeros((rows, REACH), F32)
    for h in range(2):
        high, low = split(grid[h * rows : (h + 1) * rows])
        th = t_high[h * WIDE : (h + 1) * WIDE, :]
        tl = t_low[h * WIDE : (h + 1) * WIDE, :]
        total = total + jnp.dot(high, th, preferred_element_type=F32)
        total = total + jnp.dot(low, th, preferred_element_type=F32)
        total = total + jnp.dot(high, tl, preferred_element_type=F32)
    window = total[0:ROWS]
    for quarter in range(1, QUARTERS):
        window = window + pltpu.roll(
            total[quarter * ROWS : (quarter + 1) * ROWS], quarter * PART, 1
        )
    tiles[...] = jnp.zeros(tiles.shape, F32)
    tiles[7 : 7 + ROWS, :] = window[:, 0:LANES]
    tiles[8 : 8 + ROWS, :] += window[:, LANES : 2 * LANES]
    tiles[9 : 9 + ROWS, :] += window[:, 2 * LANES : 3 * LANES]

    def copy(index, o):
        return pltpu.make_async_remote_copy(
            src_ref=tiles.at[pl.ds((3 + o) * 8, 8), :],
            dst_ref=inbox.at[pl.ds(index * 8, 8), :],
            send_sem=send_sem.at[index],
            recv_sem=recv_sem.at[index],
            device_id=((me + o) // n_dev, (me + o) % n_dev),
            device_id_type=pl.DeviceIdType.MESH,
        )

    pl.semaphore_wait(barrier, peers)
    for index, o in enumerate(OFFSETS):
        there = jnp.logical_and(me + o >= 0, me + o < devices)
        source = jnp.logical_and(me - o >= 0, me - o < devices)

        @pl.when(there)
        def _():
            copy(index, o).start()

        @pl.when(jnp.logical_not(source))
        def _():
            inbox[index * 8 : (index + 1) * 8, :] = jnp.zeros((8, LANES), F32)

    for index, o in enumerate(OFFSETS):
        source = jnp.logical_and(me - o >= 0, me - o < devices)

        @pl.when(source)
        def _():
            copy(index, o).wait_recv()

    total = tiles[24:32, :]
    for index in range(len(OFFSETS)):
        total = total + inbox[index * 8 : (index + 1) * 8, :]
    out_ref[...] = total
    for index, o in enumerate(OFFSETS):
        there = jnp.logical_and(me + o >= 0, me + o < devices)

        @pl.when(there)
        def _():
            copy(index, o).wait_send()


def solution(mesh):
    n_grp, n_dev = mesh.shape["grp"], mesh.shape["dev"]

    def body(
        line_bin, line_slot, strength, line_count, gauss_width, lorentz_width, mixing, factor
    ):
        lines = line_bin.shape[0]

        def call(*refs):
            kernel(n_grp, n_dev, *refs)

        vmem = pl.BlockSpec(memory_space=pltpu.VMEM)
        out = pl.pallas_call(
            call,
            out_shape=jax.ShapeDtypeStruct((SPAN // LANES, LANES), F32),
            in_specs=[vmem] * 8,
            out_specs=vmem,
            scratch_shapes=[
                pltpu.VMEM((SLOTS, REACH), F32),
                pltpu.VMEM((2 * WIDE, REACH), BF16),
                pltpu.VMEM((2 * WIDE, REACH), BF16),
                pltpu.VMEM((2 * TALL, lines), BF16),
                pltpu.VMEM((lines, WIDE), BF16),
                pltpu.VMEM((7 * 8, LANES), F32),
                pltpu.VMEM((6 * 8, LANES), F32),
                pltpu.SemaphoreType.DMA((6,)),
                pltpu.SemaphoreType.DMA((6,)),
            ],
            compiler_params=pltpu.CompilerParams(collective_id=0, has_side_effects=True),
            name="voigt",
        )(
            line_bin.reshape(lines // LANES, LANES),
            line_slot.reshape(lines // LANES, LANES),
            strength.reshape(lines // LANES, LANES),
            line_count.reshape(1, 1),
            gauss_width.reshape(1, SLOTS),
            lorentz_width.reshape(1, SLOTS),
            mixing.reshape(1, SLOTS),
            factor,
        )
        return out.reshape(SPAN)

    split_over = P(("grp", "dev"))
    return jax.shard_map(
        body,
        mesh=mesh,
        in_specs=(split_over,) * 4 + (P(),) * 4,
        out_specs=split_over,
        check_vma=False,
    )
```

time: 82.4 us -> 22.8 us (0.28)
  the two profiles are of different devices: /device:TPU:24 before, /device:TPU:1 now
where the time goes in v1:
time: 22.8 us; the launch traced here: 22.6 us
  Pallas kernels  20.6 us (90%)
  local copies, waits for them, and re-layouts  1.28 us (6%)
  between operations  0.66 us (3%)
    pallas_call x1, Pallas kernels, body(): pl.pallas_call(call, out_shape=jax.ShapeDtypeStruct((SPAN // LANES, LANES...  20.6 us
    unnamed x1, local copies, waits for them, and re-layouts  1.28 us

profile of v1, /device:TPU:1, one launch (start us, length us, event | category | flops | bytes accessed | tf_op | source)
XLA Modules:
  0.0 22.6 jit_solution(5984022858491414400)
XLA Ops:
  0.7 20.6 %voigt.1 = f32[8,128]{1,0:T(8,128)} custom-call(s32[16,128]{1,0:T(8,128)} %bitcast.10, s32[16,128]{1,0:T(8,128)} %bitcast.11, f32[16,128]{1,0:T(8,128)} %bitcast.12, s32[1,1]{1,0:T(1,128)} %bitcast.8.refs_3_, f32[1,32]{1,0:T(1,128)} %bitcast.13, f32[1,32]{1,0:T(1,128)} %bitcast.14, f32[1,32]{1,0:T(1,128)} %bitcast.15, f32[32,257]{1,0:T(8,128)} %refs_7_.1), custom_call_target="tpu_custom_call" | custom-call | tf_op jit(solution)/shard_map/voigt/pallas_call | solution.py:211
  21.3 1.3 %copy.11 = f32[1024]{0:T(1024)} copy(f32[1024]{0:T(1024)} %bitcast.9) | data formatting | bytes 8192

commit v2 on v1

v2 whole, which is shorter than its diff:
```python
import jax
import jax.numpy as jnp
from jax import lax
from jax.experimental import pallas as pl
from jax.experimental.pallas import tpu as pltpu
from jax.sharding import PartitionSpec as P

SLOTS = 32
WING = 128
HOP = 2
SPAN = 1024
LANES = 128
OFFSETS = (3, 2, 1, -3, -2, -1)
BF16 = jnp.bfloat16
F32 = jnp.float32
ROWS = (2 * HOP + 1) * SPAN // LANES
PART = 32
QUARTERS = LANES // PART
HALF = SLOTS // 2
WIDE = PART * HALF
REACH = 3 * LANES
CELLS = QUARTERS * ROWS
CUT = 88


def split(value):
    high = value.astype(BF16)
    low = (value - high.astype(F32)).astype(BF16)
    return high, low


def column(row):
    i = lax.broadcasted_iota(jnp.int32, (SLOTS, SLOTS), 0)
    j = lax.broadcasted_iota(jnp.int32, (SLOTS, SLOTS), 1)
    spread = jnp.where(i == j, jnp.broadcast_to(row, (SLOTS, SLOTS)), 0.0)
    return jnp.sum(spread, axis=1, keepdims=True)


def voigt_table(gauss_ref, lorentz_ref, mixing_ref, factor_ref, padded):
    padded[:, 0 : 2 * WING + 1] = factor_ref[...]
    back = LANES - 1 - lax.broadcasted_iota(jnp.int32, (SLOTS, LANES), 1)
    pieces = [
        jnp.take_along_axis(
            padded[:, c * LANES : (c + 1) * LANES], back, axis=1, mode="promise_in_bounds"
        )
        for c in (2, 1, 0)
    ]
    factor = jnp.concatenate(pieces, axis=1)
    m = lax.broadcasted_iota(jnp.int32, (SLOTS, REACH), 1)
    offset = (REACH - 1 - WING - m).astype(F32)
    square = offset * offset
    gauss_width = column(gauss_ref[...])
    lorentz_width = column(lorentz_ref[...])
    mixing = column(mixing_ref[...])
    wide = lorentz_width * lorentz_width
    lorentz = wide / (square + wide)
    gauss = jnp.exp(-square / (2.0 * gauss_width * gauss_width))
    raw = (mixing * lorentz + (1.0 - mixing) * gauss) * factor
    raw = jnp.where(m >= REACH - 1 - 2 * WING, raw, 0.0)
    return raw / jnp.sum(raw, axis=1, keepdims=True)


def conv(grid, t_high, t_low):
    rows = grid.shape[0] // 2
    total = jnp.zeros((rows, REACH), F32)
    for h in range(2):
        part = grid[h * rows : (h + 1) * rows]
        high = part.astype(BF16).astype(F32)
        both = jnp.concatenate([high, part - high], axis=0).astype(BF16)
        th = t_high[h * WIDE : (h + 1) * WIDE, :]
        tl = t_low[h * WIDE : (h + 1) * WIDE, :]
        twice = jnp.dot(both, th, preferred_element_type=F32)
        total = total + twice[0:rows] + twice[rows : 2 * rows]
        total = total + jnp.dot(high.astype(BF16), tl, preferred_element_type=F32)
    return total


def kernel(
    n_grp,
    n_dev,
    bin_hbm,
    slot_hbm,
    strength_hbm,
    count_hbm,
    gauss_hbm,
    lorentz_hbm,
    mixing_hbm,
    factor_hbm,
    own_ref,
    sum_ref,
    bin_ref,
    slot_ref,
    strength_ref,
    count_ref,
    gauss_ref,
    lorentz_ref,
    mixing_ref,
    factor_ref,
    padded,
    t_high,
    t_low,
    a_ref,
    b_ref,
    stage,
    upper,
    lower,
    inbox,
    in_sem,
    send_sem,
    recv_sem,
):
    devices = n_grp * n_dev
    dev = lax.axis_index("dev")
    me = lax.axis_index("grp") * n_dev + dev

    barrier = pltpu.get_barrier_semaphore()
    peers = jnp.int32(0)
    for o in OFFSETS:
        there = jnp.logical_and(me + o >= 0, me + o < devices)
        peers = peers + there.astype(jnp.int32)

        @pl.when(there)
        def _():
            pl.semaphore_signal(
                barrier,
                inc=1,
                device_id=((me + o) // n_dev, (me + o) % n_dev),
                device_id_type=pl.DeviceIdType.MESH,
            )

    loads = [
        pltpu.make_async_copy(source, target, in_sem.at[i])
        for i, (source, target) in enumerate(
            (
                (bin_hbm, bin_ref),
                (slot_hbm, slot_ref),
                (strength_hbm, strength_ref),
                (count_hbm, count_ref),
                (gauss_hbm, gauss_ref),
                (lorentz_hbm, lorentz_ref),
                (mixing_hbm, mixing_ref),
                (factor_hbm, factor_ref),
            )
        )
    ]
    for load in loads:
        load.start()
    padded[...] = jnp.zeros((SLOTS, REACH), F32)
    for index, o in enumerate(OFFSETS):
        source = jnp.logical_and(me - o >= 0, me - o < devices)

        @pl.when(jnp.logical_not(source))
        def _():
            inbox[index * 8 : (index + 1) * 8, :] = jnp.zeros((8, LANES), F32)

    for load in loads:
        load.wait()

    table = voigt_table(gauss_ref, lorentz_ref, mixing_ref, factor_ref, padded)
    table_high = table.astype(BF16).astype(F32)
    table_low = table - table_high
    for r in range(PART):
        for source, target in ((table_high, t_high), (table_low, t_low)):
            moved = pltpu.roll(source.astype(BF16), r + 2 * LANES + 1, 1)
            for h in range(2):
                target[h * WIDE + r * HALF : h * WIDE + (r + 1) * HALF, :] = moved[
                    h * HALF : (h + 1) * HALF
                ]

    lines = bin_ref.shape[0] * LANES
    near = bin_ref[...] - (dev - HOP) * SPAN
    slot = slot_ref[...]
    q = near // PART
    half = slot // HALF
    first = jnp.where(q >= CUT, half * (CELLS - CUT) + q - CUT, -1)
    second = jnp.where(q < CUT, half * CUT + q, -1)
    wide = (near % PART) * HALF + slot % HALF
    place = lax.broadcasted_iota(jnp.int32, near.shape, 0) * LANES + lax.broadcasted_iota(
        jnp.int32, near.shape, 1
    )
    weight = jnp.where(place < count_ref[...], strength_ref[...], 0.0)
    weight_high = weight.astype(BF16).astype(F32)
    weight_low = weight - weight_high
    wide = jnp.transpose(wide)
    wide_at = lax.broadcasted_iota(jnp.int32, (LANES, WIDE), 1).astype(jnp.int16)
    zero = jnp.zeros((16, LANES), BF16)

    def tile_of(value, k, dtype):
        return jnp.broadcast_to(value[k : k + 1, :], (16, LANES)).astype(dtype)

    def fill_a(place, base, tall):
        for k in range(lines // LANES):
            cols = slice(k * LANES, (k + 1) * LANES)
            at = tile_of(place, k, jnp.int16)
            high = tile_of(weight_high, k, BF16)
            low = tile_of(weight_low, k, BF16)
            for i in range(tall // 16):
                spot = (lax.broadcasted_iota(jnp.int32, (16, LANES), 0) + i * 16).astype(jnp.int16)
                hit = at == spot
                a_ref[base + i * 16 : base + (i + 1) * 16, cols] = jnp.where(hit, high, zero)
                a_ref[base + tall + i * 16 : base + tall + (i + 1) * 16, cols] = jnp.where(
                    hit, low, zero
                )

    def fill_b():
        for k in range(lines // LANES):
            col = jnp.broadcast_to(wide[:, k : k + 1], (LANES, WIDE)).astype(jnp.int16)
            b_ref[k * LANES : (k + 1) * LANES, :] = jnp.where(
                col == wide_at, jnp.ones((LANES, WIDE), BF16), jnp.zeros((LANES, WIDE), BF16)
            )

    def deposit(base, tall):
        both = jnp.dot(a_ref[base : base + 2 * tall, :], b_ref[...], preferred_element_type=F32)
        return both[0:tall] + both[tall : 2 * tall]

    def window(total):
        rows = total.shape[0] // QUARTERS
        for c in range(3):
            stage[c, 0 : total.shape[0], :] = total[:, c * LANES : (c + 1) * LANES]

        def every(quarter):
            return jnp.concatenate(
                [stage[c, pl.ds(quarter, rows, stride=QUARTERS), :] for c in range(3)], axis=1
            )

        value = every(0)
        for quarter in range(1, QUARTERS):
            value = value + pltpu.roll(every(quarter), quarter * PART, 1)
        return value

    def spread(target, at, value):
        rows = value.shape[0]
        target[...] = jnp.zeros(target.shape, F32)
        target[at : at + rows, :] = value[:, 0:LANES]
        target[at + 1 : at + 1 + rows, :] += value[:, LANES : 2 * LANES]
        target[at + 2 : at + 2 + rows, :] += value[:, 2 * LANES : 3 * LANES]

    def copy(index):
        o = OFFSETS[index]
        return pltpu.make_async_remote_copy(
            src_ref=upper.at[pl.ds(o * 8, 8), :] if o > 0 else lower.at[pl.ds((3 + o) * 8, 8), :],
            dst_ref=inbox.at[pl.ds(index * 8, 8), :],
            send_sem=send_sem.at[index],
            recv_sem=recv_sem.at[index],
            device_id=((me + o) // n_dev, (me + o) % n_dev),
            device_id_type=pl.DeviceIdType.MESH,
        )

    def send(index):
        o = OFFSETS[index]

        @pl.when(jnp.logical_and(me + o >= 0, me + o < devices))
        def _():
            copy(index).start()

    fill_b()
    fill_a(first, 0, 2 * (CELLS - CUT))
    far = window(conv(deposit(0, 2 * (CELLS - CUT)), t_high, t_low))
    spread(upper, (CUT // QUARTERS + 7) - 24, far)
    pl.semaphore_wait(barrier, peers)
    for index in range(3):
        send(index)

    base = 4 * (CELLS - CUT)
    fill_a(second, base, 2 * CUT)
    close = window(conv(deposit(base, 2 * CUT), t_high, t_low))
    spread(lower, 7, close)
    for index in range(3, 6):
        send(index)

    own_ref[...] = lower[24:32, :] + upper[0:8, :]
    for index, o in enumerate(OFFSETS):

        @pl.when(jnp.logical_and(me - o >= 0, me - o < devices))
        def _():
            copy(index).wait_recv()

    total = inbox[0:8, :]
    for index in range(1, len(OFFSETS)):
        total = total + inbox[index * 8 : (index + 1) * 8, :]
    sum_ref[...] = total
    for index, o in enumerate(OFFSETS):

        @pl.when(jnp.logical_and(me + o >= 0, me + o < devices))
        def _():
            copy(index).wait_send()


def solution(mesh):
    n_grp, n_dev = mesh.shape["grp"], mesh.shape["dev"]

    def body(
        line_bin, line_slot, strength, line_count, gauss_width, lorentz_width, mixing, factor
    ):
        lines = line_bin.shape[0]

        def call(*refs):
            kernel(n_grp, n_dev, *refs)

        vmem = pl.BlockSpec(memory_space=pltpu.VMEM)
        hbm = pl.BlockSpec(memory_space=pl.ANY)
        piece = jax.ShapeDtypeStruct((SPAN // LANES, LANES), F32)
        own, received = pl.pallas_call(
            call,
            out_shape=(piece, piece),
            in_specs=[hbm] * 8,
            out_specs=(vmem, vmem),
            scratch_shapes=[
                pltpu.VMEM((lines // LANES, LANES), jnp.int32),
                pltpu.VMEM((lines // LANES, LANES), jnp.int32),
                pltpu.VMEM((lines // LANES, LANES), F32),
                pltpu.VMEM((1, 1), jnp.int32),
                pltpu.VMEM((1, SLOTS), F32),
                pltpu.VMEM((1, SLOTS), F32),
                pltpu.VMEM((1, SLOTS), F32),
                pltpu.VMEM((SLOTS, 2 * WING + 1), F32),
                pltpu.VMEM((SLOTS, REACH), F32),
                pltpu.VMEM((2 * WIDE, REACH), BF16),
                pltpu.VMEM((2 * WIDE, REACH), BF16),
                pltpu.VMEM((4 * CELLS, lines), BF16),
                pltpu.VMEM((lines, WIDE), BF16),
                pltpu.VMEM((3, CUT, LANES), F32),
                pltpu.VMEM((4 * 8, LANES), F32),
                pltpu.VMEM((4 * 8, LANES), F32),
                pltpu.VMEM((6 * 8, LANES), F32),
                pltpu.SemaphoreType.DMA((8,)),
                pltpu.SemaphoreType.DMA((6,)),
                pltpu.SemaphoreType.DMA((6,)),
            ],
            compiler_params=pltpu.CompilerParams(collective_id=0, has_side_effects=True),
            name="voigt",
        )(
            line_bin.reshape(lines // LANES, LANES),
            line_slot.reshape(lines // LANES, LANES),
            strength.reshape(lines // LANES, LANES),
            line_count.reshape(1, 1),
            gauss_width.reshape(1, SLOTS),
            lorentz_width.reshape(1, SLOTS),
            mixing.reshape(1, SLOTS),
            factor,
        )
        return (own + received).reshape(SPAN)

    split_over = P(("grp", "dev"))
    return jax.shard_map(
        body,
        mesh=mesh,
        in_specs=(split_over,) * 4 + (P(),) * 4,
        out_specs=split_over,
        check_vma=False,
    )
```

time: 22.8 us -> 22 us (0.965)
  other arithmetic: 0 us -> 1.29 us
  local copies, waits for them, and re-layouts: 1.28 us -> 0 us
  Pallas kernels: 20.6 us -> 19.8 us
    reshape x0 -> x1, other arithmetic: none -> 1.29 us  [body(): return (own + received).reshape(SPAN)]
    unnamed x1 -> x0, local copies, waits for them, and re-layouts: 1.28 us -> none
    pallas_call x1, Pallas kernels: 20.6 us -> 19.8 us  [body(): pl.pallas_call(call, out_shape=(piece, piece), in_specs=[hbm] * 8, out_sp...]
where the time goes in v2:
time: 22 us; the launch traced here: 21.8 us
  Pallas kernels  19.8 us (90%)
  other arithmetic  1.29 us (6%)
  between operations  0.66 us (3%)
    pallas_call x1, Pallas kernels, body(): pl.pallas_call(call, out_shape=(piece, piece), in_specs=[hbm] * 8, out_sp...  19.8 us
    reshape x1, other arithmetic, body(): return (own + received).reshape(SPAN)  1.29 us

profile of v2, /device:TPU:1, one launch (start us, length us, event | category | flops | bytes accessed | tf_op | source)
XLA Modules:
  0.0 21.8 jit_solution(4168563388153253434)
XLA Ops:
  0.7 19.8 %voigt.1 = (f32[8,128]{1,0:T(8,128)}, f32[8,128]{1,0:T(8,128)}) custom-call(s32[16,128]{1,0:T(8,128)} %bitcast.10, s32[16,128]{1,0:T(8,128)} %bitcast.11, f32[16,128]{1,0:T(8,128)} %bitcast.12, s32[1,1]{1,0:T(1,128)} %bitcast.9.refs_3_, f32[1,32]{1,0:T(1,128)} %bitcast.13, f32[1,32]{1,0:T(1,128)} %bitcast.14, f32[1,32]{1,0:T(1,128)} %bitcast.15, ...), custom_call_target="tpu_custom_call" | custom-call | tf_op jit(solution)/shard_map/voigt/pallas_call | solution.py:303
  20.5 1.3 %add_bitcast_fusion = f32[1024]{0:T(1024)} fusion(f32[8,128]{1,0:T(8,128)} %get-tuple-element.7, f32[8,128]{1,0:T(8,128)} %get-tuple-element.8), kind=kLoop, calls=%fused_computation | loop fusion | flops 1024 | bytes 12288 | tf_op jit(solution)/shard_map/reshape | solution.py:342

commit v3 on v2

--- a/solution.py
+++ b/solution.py
@@ -14,13 +14,15 @@
 BF16 = jnp.bfloat16
 F32 = jnp.float32
 ROWS = (2 * HOP + 1) * SPAN // LANES
-PART = 32
-QUARTERS = LANES // PART
-HALF = SLOTS // 2
-WIDE = PART * HALF
+PART = 16
+SUBS = LANES // PART
+WIDE = PART * SLOTS
 REACH = 3 * LANES
-CELLS = QUARTERS * ROWS
-CUT = 88
+CELLS = SUBS * ROWS
+CUT = 176
+
+
+GRANT = 24 << 20
 
 
 def split(value):
@@ -61,18 +63,12 @@
 
 
 def conv(grid, t_high, t_low):
-    rows = grid.shape[0] // 2
-    total = jnp.zeros((rows, REACH), F32)
-    for h in range(2):
-        part = grid[h * rows : (h + 1) * rows]
-        high = part.astype(BF16).astype(F32)
-        both = jnp.concatenate([high, part - high], axis=0).astype(BF16)
-        th = t_high[h * WIDE : (h + 1) * WIDE, :]
-        tl = t_low[h * WIDE : (h + 1) * WIDE, :]
-        twice = jnp.dot(both, th, preferred_element_type=F32)
-        total = total + twice[0:rows] + twice[rows : 2 * rows]
-        total = total + jnp.dot(high.astype(BF16), tl, preferred_element_type=F32)
-    return total
+    rows = grid.shape[0]
+    high = grid.astype(BF16).astype(F32)
+    both = jnp.concatenate([high, grid - high], axis=0).astype(BF16)
+    twice = jnp.dot(both, t_high[...], preferred_element_type=F32)
+    rest = jnp.dot(high.astype(BF16), t_low[...], preferred_element_type=F32)
+    return twice[0:rows] + twice[rows : 2 * rows] + rest
 
 
 def kernel(
@@ -81,7 +77,7 @@
     bin_hbm,
     slot_hbm,
     strength_hbm,
-    count_hbm,
+    count_ref,
     gauss_hbm,
     lorentz_hbm,
     mixing_hbm,
@@ -91,7 +87,6 @@
     bin_ref,
     slot_ref,
     strength_ref,
-    count_ref,
     gauss_ref,
     lorentz_ref,
     mixing_ref,
@@ -113,21 +108,6 @@
     dev = lax.axis_index("dev")
     me = lax.axis_index("grp") * n_dev + dev
 
-    barrier = pltpu.get_barrier_semaphore()
-    peers = jnp.int32(0)
-    for o in OFFSETS:
-        there = jnp.logical_and(me + o >= 0, me + o < devices)
-        peers = peers + there.astype(jnp.int32)
-
-        @pl.when(there)
-        def _():
-            pl.semaphore_signal(
-                barrier,
-                inc=1,
-                device_id=((me + o) // n_dev, (me + o) % n_dev),
-                device_id_type=pl.DeviceIdType.MESH,
-            )
-
     loads = [
         pltpu.make_async_copy(source, target, in_sem.at[i])
         for i, (source, target) in enumerate(
@@ -135,7 +115,6 @@
                 (bin_hbm, bin_ref),
                 (slot_hbm, slot_ref),
                 (strength_hbm, strength_ref),
-                (count_hbm, count_ref),
                 (gauss_hbm, gauss_ref),
                 (lorentz_hbm, lorentz_ref),
                 (mixing_hbm, mixing_ref),
@@ -145,6 +124,21 @@
     ]
     for load in loads:
         load.start()
+    barrier = pltpu.get_barrier_semaphore()
+    peers = jnp.int32(0)
+    for o in OFFSETS:
+        there = jnp.logical_and(me + o >= 0, me + o < devices)
+        peers = peers + there.astype(jnp.int32)
+
+        @pl.when(there)
+        def _():
+            pl.semaphore_signal(
+                barrier,
+                inc=1,
+                device_id=(lax.div(me + o, n_dev), lax.rem(me + o, n_dev)),
+                device_id_type=pl.DeviceIdType.MESH,
+            )
+
     padded[...] = jnp.zeros((SLOTS, REACH), F32)
     for index, o in enumerate(OFFSETS):
         source = jnp.logical_and(me - o >= 0, me - o < devices)
@@ -157,28 +151,23 @@
         load.wait()
 
     table = voigt_table(gauss_ref, lorentz_ref, mixing_ref, factor_ref, padded)
-    table_high = table.astype(BF16).astype(F32)
-    table_low = table - table_high
+    table_high, table_low = split(table)
     for r in range(PART):
-        for source, target in ((table_high, t_high), (table_low, t_low)):
-            moved = pltpu.roll(source.astype(BF16), r + 2 * LANES + 1, 1)
-            for h in range(2):
-                target[h * WIDE + r * HALF : h * WIDE + (r + 1) * HALF, :] = moved[
-                    h * HALF : (h + 1) * HALF
-                ]
+        rows = slice(r * SLOTS, (r + 1) * SLOTS)
+        t_high[rows, :] = pltpu.roll(table_high, r + 2 * LANES + 1, 1)
+        t_low[rows, :] = pltpu.roll(table_low, r + 2 * LANES + 1, 1)
 
     lines = bin_ref.shape[0] * LANES
     near = bin_ref[...] - (dev - HOP) * SPAN
     slot = slot_ref[...]
     q = near // PART
-    half = slot // HALF
-    first = jnp.where(q >= CUT, half * (CELLS - CUT) + q - CUT, -1)
-    second = jnp.where(q < CUT, half * CUT + q, -1)
-    wide = (near % PART) * HALF + slot % HALF
+    first = jnp.where(q >= CUT, q - CUT, -1)
+    second = jnp.where(q < CUT, q, -1)
+    wide = (near % PART) * SLOTS + slot
     place = lax.broadcasted_iota(jnp.int32, near.shape, 0) * LANES + lax.broadcasted_iota(
         jnp.int32, near.shape, 1
     )
-    weight = jnp.where(place < count_ref[...], strength_ref[...], 0.0)
+    weight = jnp.where(place < count_ref[0], strength_ref[...], 0.0)
     weight_high = weight.astype(BF16).astype(F32)
     weight_low = weight - weight_high
     wide = jnp.transpose(wide)
@@ -214,18 +203,18 @@
         return both[0:tall] + both[tall : 2 * tall]
 
     def window(total):
-        rows = total.shape[0] // QUARTERS
+        rows = total.shape[0] // SUBS
         for c in range(3):
             stage[c, 0 : total.shape[0], :] = total[:, c * LANES : (c + 1) * LANES]
 
-        def every(quarter):
+        def every(sub):
             return jnp.concatenate(
-                [stage[c, pl.ds(quarter, rows, stride=QUARTERS), :] for c in range(3)], axis=1
+                [stage[c, pl.ds(sub, rows, stride=SUBS), :] for c in range(3)], axis=1
             )
 
         value = every(0)
-        for quarter in range(1, QUARTERS):
-            value = value + pltpu.roll(every(quarter), quarter * PART, 1)
+        for sub in range(1, SUBS):
+            value = value + pltpu.roll(every(sub), sub * PART, 1)
         return value
 
     def spread(target, at, value):
@@ -242,7 +231,7 @@
             dst_ref=inbox.at[pl.ds(index * 8, 8), :],
             send_sem=send_sem.at[index],
             recv_sem=recv_sem.at[index],
-            device_id=((me + o) // n_dev, (me + o) % n_dev),
+            device_id=(lax.div(me + o, n_dev), lax.rem(me + o, n_dev)),
             device_id_type=pl.DeviceIdType.MESH,
         )
 
@@ -254,16 +243,16 @@
             copy(index).start()
 
     fill_b()
-    fill_a(first, 0, 2 * (CELLS - CUT))
-    far = window(conv(deposit(0, 2 * (CELLS - CUT)), t_high, t_low))
-    spread(upper, (CUT // QUARTERS + 7) - 24, far)
+    fill_a(first, 0, CELLS - CUT)
+    far = window(conv(deposit(0, CELLS - CUT), t_high, t_low))
+    spread(upper, (CUT // SUBS + 7) - 24, far)
     pl.semaphore_wait(barrier, peers)
     for index in range(3):
         send(index)
 
-    base = 4 * (CELLS - CUT)
-    fill_a(second, base, 2 * CUT)
-    close = window(conv(deposit(base, 2 * CUT), t_high, t_low))
+    base = 2 * (CELLS - CUT)
+    fill_a(second, base, CUT)
+    close = window(conv(deposit(base, CUT), t_high, t_low))
     spread(lower, 7, close)
     for index in range(3, 6):
         send(index)
@@ -298,46 +287,52 @@
             kernel(n_grp, n_dev, *refs)
 
         vmem = pl.BlockSpec(memory_space=pltpu.VMEM)
-        hbm = pl.BlockSpec(memory_space=pl.ANY)
+        hbm = pl.BlockSpec(memory_space=pltpu.HBM)
         piece = jax.ShapeDtypeStruct((SPAN // LANES, LANES), F32)
         own, received = pl.pallas_call(
             call,
             out_shape=(piece, piece),
-            in_specs=[hbm] * 8,
+            in_specs=[hbm] * 3 + [pl.BlockSpec(memory_space=pltpu.SMEM)] + [hbm] * 4,
             out_specs=(vmem, vmem),
             scratch_shapes=[
                 pltpu.VMEM((lines // LANES, LANES), jnp.int32),
                 pltpu.VMEM((lines // LANES, LANES), jnp.int32),
                 pltpu.VMEM((lines // LANES, LANES), F32),
-                pltpu.VMEM((1, 1), jnp.int32),
                 pltpu.VMEM((1, SLOTS), F32),
                 pltpu.VMEM((1, SLOTS), F32),
                 pltpu.VMEM((1, SLOTS), F32),
                 pltpu.VMEM((SLOTS, 2 * WING + 1), F32),
                 pltpu.VMEM((SLOTS, REACH), F32),
-                pltpu.VMEM((2 * WIDE, REACH), BF16),
-                pltpu.VMEM((2 * WIDE, REACH), BF16),
-                pltpu.VMEM((4 * CELLS, lines), BF16),
+                pltpu.VMEM((WIDE, REACH), BF16),
+                pltpu.VMEM((WIDE, REACH), BF16),
+                pltpu.VMEM((2 * CELLS, lines), BF16),
                 pltpu.VMEM((lines, WIDE), BF16),
                 pltpu.VMEM((3, CUT, LANES), F32),
                 pltpu.VMEM((4 * 8, LANES), F32),
                 pltpu.VMEM((4 * 8, LANES), F32),
                 pltpu.VMEM((6 * 8, LANES), F32),
-                pltpu.SemaphoreType.DMA((8,)),
+                pltpu.SemaphoreType.DMA((7,)),
                 pltpu.SemaphoreType.DMA((6,)),
                 pltpu.SemaphoreType.DMA((6,)),
             ],
-            compiler_params=pltpu.CompilerParams(collective_id=0, has_side_effects=True),
+            compiler_params=pltpu.CompilerParams(
+                collective_id=0, has_side_effects=True, vmem_limit_bytes=GRANT
+            ),
             name="voigt",
         )(
-            line_bin.reshape(lines // LANES, LANES),
-            line_slot.reshape(lines // LANES, LANES),
-            strength.reshape(lines // LANES, LANES),
-            line_count.reshape(1, 1),
-            gauss_width.reshape(1, SLOTS),
-            lorentz_width.reshape(1, SLOTS),
-            mixing.reshape(1, SLOTS),
-            factor,
+            *(
+                value if value.size == 1 else pltpu.with_memory_space_constraint(value, pltpu.HBM)
+                for value in (
+                    line_bin.reshape(lines // LANES, LANES),
+                    line_slot.reshape(lines // LANES, LANES),
+                    strength.reshape(lines // LANES, LANES),
+                    line_count,
+                    gauss_width.reshape(1, SLOTS),
+                    lorentz_width.reshape(1, SLOTS),
+                    mixing.reshape(1, SLOTS),
+                    factor,
+                )
+            )
         )
         return (own + received).reshape(SPAN)
 

time: 22 us -> 20.7 us (0.941)
  other arithmetic: 1.29 us -> 0.6 us
  Pallas kernels: 19.8 us -> 19.2 us
    reshape x1, other arithmetic: 1.29 us -> 0.6 us  [body(): return (own + received).reshape(SPAN)]
    pallas_call x1, Pallas kernels: 19.8 us -> 19.2 us  [body(): pl.pallas_call(call, out_shape=(piece, piece), in_specs=[hbm] * 3 + [pl.B...]
where the time goes in v3:
time: 20.7 us; the launch traced here: 20.5 us
  Pallas kernels  19.2 us (93%)
  between operations  0.66 us (3%)
  other arithmetic  0.6 us (3%)
    pallas_call x1, Pallas kernels, body(): pl.pallas_call(call, out_shape=(piece, piece), in_specs=[hbm] * 3 + [pl.B...  19.2 us
    reshape x1, other arithmetic, body(): return (own + received).reshape(SPAN)  0.6 us

profile of v3, /device:TPU:1, one launch (start us, length us, event | category | flops | bytes accessed | tf_op | source)
XLA Modules:
  0.0 20.5 jit_solution(1212440482448804782)
XLA Ops:
  0.7 19.2 %voigt.1 = (f32[8,128]{1,0:T(8,128)S(1)}, f32[8,128]{1,0:T(8,128)S(1)}) custom-call(s32[16,128]{1,0:T(8,128)} %bitcast.8, s32[16,128]{1,0:T(8,128)} %bitcast.9, f32[16,128]{1,0:T(8,128)} %bitcast.10, s32[1]{0:T(128)S(6)} %copy.9.refs_3_, f32[1,32]{1,0:T(1,128)} %bitcast.11, f32[1,32]{1,0:T(1,128)} %bitcast.12, f32[1,32]{1,0:T(1,128)} %bitcast.13, ...), custom_call_target="tpu_custom_call" | custom-call | tf_op jit(solution)/shard_map/voigt/pallas_call | solution.py:292
  19.9 0.6 %add_bitcast_fusion = f32[1024]{0:T(1024)} fusion(f32[8,128]{1,0:T(8,128)S(1)} %get-tuple-element.7, f32[8,128]{1,0:T(8,128)S(1)} %get-tuple-element.8), kind=kLoop, calls=%fused_computation | loop fusion | flops 1024 | bytes 12288 | tf_op jit(solution)/shard_map/reshape | solution.py:337

commit v4 on v3

--- a/solution.py
+++ b/solution.py
@@ -19,7 +19,7 @@
 WIDE = PART * SLOTS
 REACH = 3 * LANES
 CELLS = SUBS * ROWS
-CUT = 176
+MID = 184
 
 
 GRANT = 24 << 20
@@ -94,8 +94,6 @@
     padded,
     t_high,
     t_low,
-    a_ref,
-    b_ref,
     stage,
     upper,
     lower,
@@ -103,6 +101,7 @@
     in_sem,
     send_sem,
     recv_sem,
+    ready_sem,
 ):
     devices = n_grp * n_dev
     dev = lax.axis_index("dev")
@@ -124,26 +123,27 @@
     ]
     for load in loads:
         load.start()
-    barrier = pltpu.get_barrier_semaphore()
-    peers = jnp.int32(0)
-    for o in OFFSETS:
-        there = jnp.logical_and(me + o >= 0, me + o < devices)
-        peers = peers + there.astype(jnp.int32)
-
-        @pl.when(there)
+    def exists(o):
+        return me + o < devices if o > 0 else me + o >= 0
+
+    def tell(semaphore, o):
+        @pl.when(exists(o))
         def _():
             pl.semaphore_signal(
-                barrier,
+                semaphore,
                 inc=1,
                 device_id=(lax.div(me + o, n_dev), lax.rem(me + o, n_dev)),
                 device_id_type=pl.DeviceIdType.MESH,
             )
 
+    barrier = pltpu.get_barrier_semaphore()
+    above = jnp.int32(0)
+    for o in (1, 2, 3):
+        above = above + exists(o).astype(jnp.int32)
+        tell(barrier, -o)
     padded[...] = jnp.zeros((SLOTS, REACH), F32)
     for index, o in enumerate(OFFSETS):
-        source = jnp.logical_and(me - o >= 0, me - o < devices)
-
-        @pl.when(jnp.logical_not(source))
+        @pl.when(jnp.logical_not(exists(-o)))
         def _():
             inbox[index * 8 : (index + 1) * 8, :] = jnp.zeros((8, LANES), F32)
 
@@ -161,8 +161,6 @@
     near = bin_ref[...] - (dev - HOP) * SPAN
     slot = slot_ref[...]
     q = near // PART
-    first = jnp.where(q >= CUT, q - CUT, -1)
-    second = jnp.where(q < CUT, q, -1)
     wide = (near % PART) * SLOTS + slot
     place = lax.broadcasted_iota(jnp.int32, near.shape, 0) * LANES + lax.broadcasted_iota(
         jnp.int32, near.shape, 1
@@ -171,36 +169,64 @@
     weight_high = weight.astype(BF16).astype(F32)
     weight_low = weight - weight_high
     wide = jnp.transpose(wide)
-    wide_at = lax.broadcasted_iota(jnp.int32, (LANES, WIDE), 1).astype(jnp.int16)
+    lane = lax.broadcasted_iota(jnp.int32, (LANES, LANES), 1)
+    spot = lax.broadcasted_iota(jnp.int32, (16, LANES), 0)
+    blocks = lines // LANES
     zero = jnp.zeros((16, LANES), BF16)
 
     def tile_of(value, k, dtype):
         return jnp.broadcast_to(value[k : k + 1, :], (16, LANES)).astype(dtype)
 
-    def fill_a(place, base, tall):
-        for k in range(lines // LANES):
-            cols = slice(k * LANES, (k + 1) * LANES)
+    def column_of(k):
+        return jnp.broadcast_to(wide[:, k : k + 1], (LANES, LANES)).astype(jnp.int16)
+
+    def one_hot():
+        rows = []
+        for k in range(blocks):
+            at = column_of(k)
+            rows.append(
+                jnp.concatenate(
+                    [
+                        jnp.where(
+                            at == (lane + c * LANES).astype(jnp.int16),
+                            jnp.ones((LANES, LANES), BF16),
+                            jnp.zeros((LANES, LANES), BF16),
+                        )
+                        for c in range(WIDE // LANES)
+                    ],
+                    axis=1,
+                )
+            )
+        return jnp.concatenate(rows, axis=0)
+
+    def weighted(low_cell, high_cell):
+        rows = high_cell - low_cell
+        inside = jnp.logical_and(q >= low_cell, q < high_cell)
+        place = jnp.where(inside, q - low_cell, -4 * CELLS)
+        cols = []
+        for k in range(blocks):
             at = tile_of(place, k, jnp.int16)
+            at_low = tile_of(place + rows, k, jnp.int16)
             high = tile_of(weight_high, k, BF16)
             low = tile_of(weight_low, k, BF16)
-            for i in range(tall // 16):
-                spot = (lax.broadcasted_iota(jnp.int32, (16, LANES), 0) + i * 16).astype(jnp.int16)
-                hit = at == spot
-                a_ref[base + i * 16 : base + (i + 1) * 16, cols] = jnp.where(hit, high, zero)
-                a_ref[base + tall + i * 16 : base + tall + (i + 1) * 16, cols] = jnp.where(
-                    hit, low, zero
-                )
-
-    def fill_b():
-        for k in range(lines // LANES):
-            col = jnp.broadcast_to(wide[:, k : k + 1], (LANES, WIDE)).astype(jnp.int16)
-            b_ref[k * LANES : (k + 1) * LANES, :] = jnp.where(
-                col == wide_at, jnp.ones((LANES, WIDE), BF16), jnp.zeros((LANES, WIDE), BF16)
-            )
-
-    def deposit(base, tall):
-        both = jnp.dot(a_ref[base : base + 2 * tall, :], b_ref[...], preferred_element_type=F32)
-        return both[0:tall] + both[tall : 2 * tall]
+            tiles = []
+            for i in range(2 * rows // 16):
+                here = (spot + i * 16).astype(jnp.int16)
+                value = zero
+                if (i + 1) * 16 > rows:
+                    value = jnp.where(at_low == here, low, value)
+                if i * 16 < rows:
+                    value = jnp.where(at == here, high, value)
+                tiles.append(value)
+            cols.append(jnp.concatenate(tiles, axis=0))
+        return jnp.concatenate(cols, axis=1)
+
+    def deposit(low_cell, high_cell):
+        rows = high_cell - low_cell
+        both = jnp.dot(
+            weighted(low_cell, high_cell), one_hot(), preferred_element_type=F32
+        )
+        return both[0:rows] + both[rows : 2 * rows]
 
     def window(total):
         rows = total.shape[0] // SUBS
@@ -224,10 +250,14 @@
         target[at + 1 : at + 1 + rows, :] += value[:, LANES : 2 * LANES]
         target[at + 2 : at + 2 + rows, :] += value[:, 2 * LANES : 3 * LANES]
 
+    pieces = tuple(upper.at[pl.ds(i * 8, 8), :] for i in (3, 2, 1)) + tuple(
+        lower.at[pl.ds(i * 8, 8), :] for i in range(3)
+    )
+
     def copy(index):
         o = OFFSETS[index]
         return pltpu.make_async_remote_copy(
-            src_ref=upper.at[pl.ds(o * 8, 8), :] if o > 0 else lower.at[pl.ds((3 + o) * 8, 8), :],
+            src_ref=pieces[index],
             dst_ref=inbox.at[pl.ds(index * 8, 8), :],
             send_sem=send_sem.at[index],
             recv_sem=recv_sem.at[index],
@@ -236,31 +266,33 @@
         )
 
     def send(index):
-        o = OFFSETS[index]
-
-        @pl.when(jnp.logical_and(me + o >= 0, me + o < devices))
+        @pl.when(exists(OFFSETS[index]))
         def _():
             copy(index).start()
 
-    fill_b()
-    fill_a(first, 0, CELLS - CUT)
-    far = window(conv(deposit(0, CELLS - CUT), t_high, t_low))
-    spread(upper, (CUT // SUBS + 7) - 24, far)
-    pl.semaphore_wait(barrier, peers)
+    spread(upper, 6, window(conv(deposit(MID, CELLS), t_high, t_low)))
+    @pl.when(exists(1))
+    def _():
+        pl.semaphore_wait(barrier, above)
+
     for index in range(3):
         send(index)
-
-    base = 2 * (CELLS - CUT)
-    fill_a(second, base, CUT)
-    close = window(conv(deposit(base, CUT), t_high, t_low))
-    spread(lower, 7, close)
+    for o in (1, 2, 3):
+        tell(ready_sem.at[o - 1], o)
+
+    spread(lower, 7, window(conv(deposit(0, MID), t_high, t_low)))
+    own_ref[...] = lower[24:32, :] + upper[0:8, :]
     for index in range(3, 6):
-        send(index)
-
-    own_ref[...] = lower[24:32, :] + upper[0:8, :]
+        o = OFFSETS[index]
+
+        @pl.when(exists(o))
+        def _():
+            pl.semaphore_wait(ready_sem.at[-o - 1], 1)
+            copy(index).start()
+
     for index, o in enumerate(OFFSETS):
 
-        @pl.when(jnp.logical_and(me - o >= 0, me - o < devices))
+        @pl.when(exists(-o))
         def _():
             copy(index).wait_recv()
 
@@ -270,7 +302,7 @@
     sum_ref[...] = total
     for index, o in enumerate(OFFSETS):
 
-        @pl.when(jnp.logical_and(me + o >= 0, me + o < devices))
+        @pl.when(exists(o))
         def _():
             copy(index).wait_send()
 
@@ -305,15 +337,14 @@
                 pltpu.VMEM((SLOTS, REACH), F32),
                 pltpu.VMEM((WIDE, REACH), BF16),
                 pltpu.VMEM((WIDE, REACH), BF16),
-                pltpu.VMEM((2 * CELLS, lines), BF16),
-                pltpu.VMEM((lines, WIDE), BF16),
-                pltpu.VMEM((3, CUT, LANES), F32),
+                pltpu.VMEM((3, MID, LANES), F32),
                 pltpu.VMEM((4 * 8, LANES), F32),
                 pltpu.VMEM((4 * 8, LANES), F32),
                 pltpu.VMEM((6 * 8, LANES), F32),
                 pltpu.SemaphoreType.DMA((7,)),
                 pltpu.SemaphoreType.DMA((6,)),
                 pltpu.SemaphoreType.DMA((6,)),
+                pltpu.SemaphoreType.REGULAR((3,)),
             ],
             compiler_params=pltpu.CompilerParams(
                 collective_id=0, has_side_effects=True, vmem_limit_bytes=GRANT

time: 20.7 us -> 20.9 us (level)
  no operation moved by 1% of the time
where the time goes in v4:
time: 20.9 us; the launch traced here: 20.7 us
  Pallas kernels  19.4 us (93%)
  between operations  0.66 us (3%)
  other arithmetic  0.6 us (3%)
    pallas_call x1, Pallas kernels, body(): pl.pallas_call(call, out_shape=(piece, piece), in_specs=[hbm] * 3 + [pl.B...  19.4 us
    reshape x1, other arithmetic, body(): return (own + received).reshape(SPAN)  0.6 us

profile of v4, /device:TPU:1, one launch (start us, length us, event | category | flops | bytes accessed | tf_op | source)
XLA Modules:
  0.0 20.7 jit_solution(8742306379487595772)
XLA Ops:
  0.7 19.4 %voigt.1 = (f32[8,128]{1,0:T(8,128)S(1)}, f32[8,128]{1,0:T(8,128)S(1)}) custom-call(s32[16,128]{1,0:T(8,128)} %bitcast.8, s32[16,128]{1,0:T(8,128)} %bitcast.9, f32[16,128]{1,0:T(8,128)} %bitcast.10, s32[1]{0:T(128)S(6)} %copy.9.refs_3_, f32[1,32]{1,0:T(1,128)} %bitcast.11, f32[1,32]{1,0:T(1,128)} %bitcast.12, f32[1,32]{1,0:T(1,128)} %bitcast.13, ...), custom_call_target="tpu_custom_call" | custom-call | tf_op jit(solution)/shard_map/voigt/pallas_call | solution.py:324
  20.1 0.6 %add_bitcast_fusion = f32[1024]{0:T(1024)} fusion(f32[8,128]{1,0:T(8,128)S(1)} %get-tuple-element.7, f32[8,128]{1,0:T(8,128)S(1)} %get-tuple-element.8), kind=kLoop, calls=%fused_computation | loop fusion | flops 1024 | bytes 12288 | tf_op jit(solution)/shard_map/reshape | solution.py:368

commit v5 on v4

--- a/solution.py
+++ b/solution.py
@@ -10,7 +10,9 @@
 HOP = 2
 SPAN = 1024
 LANES = 128
-OFFSETS = (3, 2, 1, -3, -2, -1)
+ROW = 16
+OFFSETS = (3, 2, 1, -2, -1)
+SPOTS = ((0, 8), (8, 8), (16, 8), (24, 16), (40, 8))
 BF16 = jnp.bfloat16
 F32 = jnp.float32
 ROWS = (2 * HOP + 1) * SPAN // LANES
@@ -19,6 +21,7 @@
 WIDE = PART * SLOTS
 REACH = 3 * LANES
 CELLS = SUBS * ROWS
+FAR = 248
 MID = 184
 
 
@@ -94,14 +97,17 @@
     padded,
     t_high,
     t_low,
+    wide_ref,
     stage,
-    upper,
+    far,
+    middle,
+    near_up,
+    near_down,
     lower,
     inbox,
     in_sem,
     send_sem,
     recv_sem,
-    ready_sem,
 ):
     devices = n_grp * n_dev
     dev = lax.axis_index("dev")
@@ -123,6 +129,8 @@
     ]
     for load in loads:
         load.start()
+    late = lax.rem(dev, ROW) >= ROW // 2
+
     def exists(o):
         return me + o < devices if o > 0 else me + o >= 0
 
@@ -137,15 +145,17 @@
             )
 
     barrier = pltpu.get_barrier_semaphore()
-    above = jnp.int32(0)
-    for o in (1, 2, 3):
-        above = above + exists(o).astype(jnp.int32)
+    heard = jnp.int32(0)
+    for o in OFFSETS:
+        heard = heard + exists(o).astype(jnp.int32)
         tell(barrier, -o)
+
     padded[...] = jnp.zeros((SLOTS, REACH), F32)
     for index, o in enumerate(OFFSETS):
         @pl.when(jnp.logical_not(exists(-o)))
         def _():
-            inbox[index * 8 : (index + 1) * 8, :] = jnp.zeros((8, LANES), F32)
+            at, rows = SPOTS[index]
+            inbox[at : at + rows, :] = jnp.zeros((rows, LANES), F32)
 
     for load in loads:
         load.wait()
@@ -177,10 +187,15 @@
     def tile_of(value, k, dtype):
         return jnp.broadcast_to(value[k : k + 1, :], (16, LANES)).astype(dtype)
 
-    def column_of(k):
+    wide_ref[...] = wide
+
+    def columns(k):
         return jnp.broadcast_to(wide[:, k : k + 1], (LANES, LANES)).astype(jnp.int16)
 
-    def one_hot():
+    def kept(k):
+        return jnp.broadcast_to(wide_ref[:, k : k + 1], (LANES, LANES)).astype(jnp.int16)
+
+    def one_hot(column_of):
         rows = []
         for k in range(blocks):
             at = column_of(k)
@@ -221,10 +236,10 @@
             cols.append(jnp.concatenate(tiles, axis=0))
         return jnp.concatenate(cols, axis=1)
 
-    def deposit(low_cell, high_cell):
+    def deposit(low_cell, high_cell, column_of):
         rows = high_cell - low_cell
         both = jnp.dot(
-            weighted(low_cell, high_cell), one_hot(), preferred_element_type=F32
+            weighted(low_cell, high_cell), one_hot(column_of), preferred_element_type=F32
         )
         return both[0:rows] + both[rows : 2 * rows]
 
@@ -250,55 +265,62 @@
         target[at + 1 : at + 1 + rows, :] += value[:, LANES : 2 * LANES]
         target[at + 2 : at + 2 + rows, :] += value[:, 2 * LANES : 3 * LANES]
 
-    pieces = tuple(upper.at[pl.ds(i * 8, 8), :] for i in (3, 2, 1)) + tuple(
-        lower.at[pl.ds(i * 8, 8), :] for i in range(3)
-    )
+    pieces = (far.at[pl.ds(16, 8), :], far.at[pl.ds(8, 8), :], near_up)
+    pieces += (lower.at[pl.ds(0, 16), :], near_down)
 
     def copy(index):
         o = OFFSETS[index]
         return pltpu.make_async_remote_copy(
             src_ref=pieces[index],
-            dst_ref=inbox.at[pl.ds(index * 8, 8), :],
+            dst_ref=inbox.at[pl.ds(*SPOTS[index]), :],
             send_sem=send_sem.at[index],
             recv_sem=recv_sem.at[index],
             device_id=(lax.div(me + o, n_dev), lax.rem(me + o, n_dev)),
             device_id_type=pl.DeviceIdType.MESH,
         )
 
-    def send(index):
-        @pl.when(exists(OFFSETS[index]))
+    def send(index, condition):
+        @pl.when(jnp.logical_and(exists(OFFSETS[index]), condition))
         def _():
             copy(index).start()
 
-    spread(upper, 6, window(conv(deposit(MID, CELLS), t_high, t_low)))
-    @pl.when(exists(1))
+    spread(far, 6, window(conv(deposit(FAR, CELLS, columns), t_high, t_low)))
+
+    @pl.when(late)
     def _():
-        pl.semaphore_wait(barrier, above)
-
-    for index in range(3):
-        send(index)
-    for o in (1, 2, 3):
-        tell(ready_sem.at[o - 1], o)
-
-    spread(lower, 7, window(conv(deposit(0, MID), t_high, t_low)))
-    own_ref[...] = lower[24:32, :] + upper[0:8, :]
-    for index in range(3, 6):
-        o = OFFSETS[index]
-
-        @pl.when(exists(o))
-        def _():
-            pl.semaphore_wait(ready_sem.at[-o - 1], 1)
-            copy(index).start()
-
-    for index, o in enumerate(OFFSETS):
-
-        @pl.when(exists(-o))
+        pl.semaphore_wait(barrier, heard)
+
+    send(0, late)
+    send(1, late)
+
+    spread(middle, 6, window(conv(deposit(MID, FAR, kept), t_high, t_low)))
+    near_up[...] = middle[8:16, :] + far[0:8, :]
+    send(2, late)
+
+    spread(lower, 7, window(conv(deposit(0, MID, kept), t_high, t_low)))
+    own_ref[...] = lower[24:32, :] + middle[0:8, :]
+    def take(index):
+        @pl.when(exists(-OFFSETS[index]))
         def _():
             copy(index).wait_recv()
 
+
+    @pl.when(jnp.logical_not(late))
+    def _():
+        pl.semaphore_wait(barrier, heard)
+
+    for index in range(3):
+        send(index, jnp.logical_not(late))
+    send(3, True)
+    take(3)
+    near_down[...] = lower[16:24, :] + inbox[24:32, :]
+    send(4, True)
+    for index in (4, 2, 1, 0):
+        take(index)
+
     total = inbox[0:8, :]
-    for index in range(1, len(OFFSETS)):
-        total = total + inbox[index * 8 : (index + 1) * 8, :]
+    for at in (8, 16, 32, 40):
+        total = total + inbox[at : at + 8, :]
     sum_ref[...] = total
     for index, o in enumerate(OFFSETS):
 
@@ -337,14 +359,17 @@
                 pltpu.VMEM((SLOTS, REACH), F32),
                 pltpu.VMEM((WIDE, REACH), BF16),
                 pltpu.VMEM((WIDE, REACH), BF16),
+                pltpu.VMEM((LANES, lines // LANES), jnp.int32),
                 pltpu.VMEM((3, MID, LANES), F32),
-                pltpu.VMEM((4 * 8, LANES), F32),
+                pltpu.VMEM((3 * 8, LANES), F32),
+                pltpu.VMEM((2 * 8, LANES), F32),
+                pltpu.VMEM((8, LANES), F32),
+                pltpu.VMEM((8, LANES), F32),
                 pltpu.VMEM((4 * 8, LANES), F32),
                 pltpu.VMEM((6 * 8, LANES), F32),
                 pltpu.SemaphoreType.DMA((7,)),
-                pltpu.SemaphoreType.DMA((6,)),
-                pltpu.SemaphoreType.DMA((6,)),
-                pltpu.SemaphoreType.REGULAR((3,)),
+                pltpu.SemaphoreType.DMA((5,)),
+                pltpu.SemaphoreType.DMA((5,)),
             ],
             compiler_params=pltpu.CompilerParams(
                 collective_id=0, has_side_effects=True, vmem_limit_bytes=GRANT

time: 20.9 us -> 20.2 us (0.967)
  Pallas kernels: 19.4 us -> 18.8 us
    pallas_call x1, Pallas kernels: 19.4 us -> 18.8 us  [body(): pl.pallas_call(call, out_shape=(piece, piece), in_specs=[hbm] * 3 + [pl.B...]
where the time goes in v5:
time: 20.2 us; the launch traced here: 20 us
  Pallas kernels  18.8 us (93%)
  between operations  0.66 us (3%)
  other arithmetic  0.6 us (3%)
    pallas_call x1, Pallas kernels, body(): pl.pallas_call(call, out_shape=(piece, piece), in_specs=[hbm] * 3 + [pl.B...  18.8 us
    reshape x1, other arithmetic, body(): return (own + received).reshape(SPAN)  0.6 us

profile of v5, /device:TPU:1, one launch (start us, length us, event | category | flops | bytes accessed | tf_op | source)
XLA Modules:
  0.0 20.0 jit_solution(70389718501953112)
XLA Ops:
  0.7 18.8 %voigt.1 = (f32[8,128]{1,0:T(8,128)S(1)}, f32[8,128]{1,0:T(8,128)S(1)}) custom-call(s32[16,128]{1,0:T(8,128)} %bitcast.8, s32[16,128]{1,0:T(8,128)} %bitcast.9, f32[16,128]{1,0:T(8,128)} %bitcast.10, s32[1]{0:T(128)S(6)} %copy.9.refs_3_, f32[1,32]{1,0:T(1,128)} %bitcast.11, f32[1,32]{1,0:T(1,128)} %bitcast.12, f32[1,32]{1,0:T(1,128)} %bitcast.13, ...), custom_call_target="tpu_custom_call" | custom-call | tf_op jit(solution)/shard_map/voigt/pallas_call | solution.py:346
  19.4 0.6 %add_bitcast_fusion = f32[1024]{0:T(1024)} fusion(f32[8,128]{1,0:T(8,128)S(1)} %get-tuple-element.7, f32[8,128]{1,0:T(8,128)S(1)} %get-tuple-element.8), kind=kLoop, calls=%fused_computation | loop fusion | flops 1024 | bytes 12288 | tf_op jit(solution)/shard_map/reshape | solution.py:393

commit v6 on v5

--- a/solution.py
+++ b/solution.py
@@ -108,6 +108,7 @@
     in_sem,
     send_sem,
     recv_sem,
+    relay_sem,
 ):
     devices = n_grp * n_dev
     dev = lax.axis_index("dev")
@@ -129,13 +130,14 @@
     ]
     for load in loads:
         load.start()
-    late = lax.rem(dev, ROW) >= ROW // 2
+    z = lax.rem(dev, ROW)
+    late = z >= ROW // 2
 
     def exists(o):
         return me + o < devices if o > 0 else me + o >= 0
 
-    def tell(semaphore, o):
-        @pl.when(exists(o))
+    def tell(semaphore, condition, o):
+        @pl.when(condition)
         def _():
             pl.semaphore_signal(
                 semaphore,
@@ -145,10 +147,13 @@
             )
 
     barrier = pltpu.get_barrier_semaphore()
-    heard = jnp.int32(0)
-    for o in OFFSETS:
+    crosses = z >= ROW - 2
+    heard = ((exists(2) & crosses) | (exists(-2) & (z == 0))).astype(jnp.int32)
+    tell(barrier, exists(-2) & (z < 2), -2)
+    tell(barrier, exists(2) & (z == ROW - 2), 2)
+    for o in (3, 1, -1):
         heard = heard + exists(o).astype(jnp.int32)
-        tell(barrier, -o)
+        tell(barrier, exists(-o), -o)
 
     padded[...] = jnp.zeros((SLOTS, REACH), F32)
     for index, o in enumerate(OFFSETS):
@@ -157,15 +162,8 @@
             at, rows = SPOTS[index]
             inbox[at : at + rows, :] = jnp.zeros((rows, LANES), F32)
 
-    for load in loads:
+    for load in loads[:3]:
         load.wait()
-
-    table = voigt_table(gauss_ref, lorentz_ref, mixing_ref, factor_ref, padded)
-    table_high, table_low = split(table)
-    for r in range(PART):
-        rows = slice(r * SLOTS, (r + 1) * SLOTS)
-        t_high[rows, :] = pltpu.roll(table_high, r + 2 * LANES + 1, 1)
-        t_low[rows, :] = pltpu.roll(table_low, r + 2 * LANES + 1, 1)
 
     lines = bin_ref.shape[0] * LANES
     near = bin_ref[...] - (dev - HOP) * SPAN
@@ -179,6 +177,16 @@
     weight_high = weight.astype(BF16).astype(F32)
     weight_low = weight - weight_high
     wide = jnp.transpose(wide)
+    for load in loads[3:]:
+        load.wait()
+
+    table = voigt_table(gauss_ref, lorentz_ref, mixing_ref, factor_ref, padded)
+    table_high, table_low = split(table)
+    for r in range(PART):
+        rows = slice(r * SLOTS, (r + 1) * SLOTS)
+        t_high[rows, :] = pltpu.roll(table_high, r + 2 * LANES + 1, 1)
+        t_low[rows, :] = pltpu.roll(table_low, r + 2 * LANES + 1, 1)
+
     lane = lax.broadcasted_iota(jnp.int32, (LANES, LANES), 1)
     spot = lax.broadcasted_iota(jnp.int32, (16, LANES), 0)
     blocks = lines // LANES
@@ -284,14 +292,18 @@
         def _():
             copy(index).start()
 
+    def greet(condition):
+        @pl.when(condition)
+        def _():
+            pl.semaphore_wait(barrier, heard)
+
+        tell(relay_sem.at[0], condition & (z > 0) & (z < ROW - 1), -1)
+        tell(relay_sem.at[1], condition & exists(-1) & (z < ROW - 1), 1)
+
     spread(far, 6, window(conv(deposit(FAR, CELLS, columns), t_high, t_low)))
-
-    @pl.when(late)
-    def _():
-        pl.semaphore_wait(barrier, heard)
-
+    greet(late)
     send(0, late)
-    send(1, late)
+    send(1, crosses)
 
     spread(middle, 6, window(conv(deposit(MID, FAR, kept), t_high, t_low)))
     near_up[...] = middle[8:16, :] + far[0:8, :]
@@ -304,17 +316,28 @@
         def _():
             copy(index).wait_recv()
 
-
-    @pl.when(jnp.logical_not(late))
-    def _():
-        pl.semaphore_wait(barrier, heard)
-
-    for index in range(3):
-        send(index, jnp.logical_not(late))
-    send(3, True)
+    greet(jnp.logical_not(late))
+    send(0, jnp.logical_not(late))
+    send(2, jnp.logical_not(late))
+
+    def send_down(condition):
+        @pl.when(condition & exists(-2) & (z > 0))
+        def _():
+            pl.semaphore_wait(relay_sem.at[1], 1)
+
+        send(3, condition)
+
+    send_down(z >= 2)
     take(3)
     near_down[...] = lower[16:24, :] + inbox[24:32, :]
     send(4, True)
+    send_down(z < 2)
+
+    @pl.when(jnp.logical_not(crosses))
+    def _():
+        pl.semaphore_wait(relay_sem.at[0], 1)
+
+    send(1, jnp.logical_not(crosses))
     for index in (4, 2, 1, 0):
         take(index)
 
@@ -370,6 +393,7 @@
                 pltpu.SemaphoreType.DMA((7,)),
                 pltpu.SemaphoreType.DMA((5,)),
                 pltpu.SemaphoreType.DMA((5,)),
+                pltpu.SemaphoreType.REGULAR((2,)),
             ],
             compiler_params=pltpu.CompilerParams(
                 collective_id=0, has_side_effects=True, vmem_limit_bytes=GRANT

time: 20.2 us -> 19.6 us (0.970)
  Pallas kernels: 18.8 us -> 18.2 us
    pallas_call x1, Pallas kernels: 18.8 us -> 18.2 us  [body(): pl.pallas_call(call, out_shape=(piece, piece), in_specs=[hbm] * 3 + [pl.B...]
where the time goes in v6:
time: 19.6 us; the launch traced here: 19.4 us
  Pallas kernels  18.2 us (93%)
  between operations  0.66 us (3%)
  other arithmetic  0.6 us (3%)
    pallas_call x1, Pallas kernels, body(): pl.pallas_call(call, out_shape=(piece, piece), in_specs=[hbm] * 3 + [pl.B...  18.2 us
    reshape x1, other arithmetic, body(): return (own + received).reshape(SPAN)  0.6 us

profile of v6, /device:TPU:1, one launch (start us, length us, event | category | flops | bytes accessed | tf_op | source)
XLA Modules:
  0.0 19.4 jit_solution(13140668980374355751)
XLA Ops:
  0.7 18.2 %voigt.1 = (f32[8,128]{1,0:T(8,128)S(1)}, f32[8,128]{1,0:T(8,128)S(1)}) custom-call(s32[16,128]{1,0:T(8,128)} %bitcast.8, s32[16,128]{1,0:T(8,128)} %bitcast.9, f32[16,128]{1,0:T(8,128)} %bitcast.10, s32[1]{0:T(128)S(6)} %copy.9.refs_3_, f32[1,32]{1,0:T(1,128)} %bitcast.11, f32[1,32]{1,0:T(1,128)} %bitcast.12, f32[1,32]{1,0:T(1,128)} %bitcast.13, ...), custom_call_target="tpu_custom_call" | custom-call | tf_op jit(solution)/shard_map/voigt/pallas_call | solution.py:369
  18.8 0.6 %add_bitcast_fusion = f32[1024]{0:T(1024)} fusion(f32[8,128]{1,0:T(8,128)S(1)} %get-tuple-element.7, f32[8,128]{1,0:T(8,128)S(1)} %get-tuple-element.8), kind=kLoop, calls=%fused_computation | loop fusion | flops 1024 | bytes 12288 | tf_op jit(solution)/shard_map/reshape | solution.py:417

commit v7 on v6

--- a/solution.py
+++ b/solution.py
@@ -195,13 +195,19 @@
     def tile_of(value, k, dtype):
         return jnp.broadcast_to(value[k : k + 1, :], (16, LANES)).astype(dtype)
 
-    wide_ref[...] = wide
+    pairs = wide[:, 0:(blocks // 2)] + wide[:, (blocks // 2) : 2 * (blocks // 2)] * 65536
+    wide_ref[...] = pairs
+
+    def unpack(words, k):
+        word = words[:, k % (blocks // 2) : k % (blocks // 2) + 1]
+        word = jnp.broadcast_to(word, (LANES, LANES))
+        return (word if k < (blocks // 2) else word >> 16).astype(jnp.int16)
 
     def columns(k):
-        return jnp.broadcast_to(wide[:, k : k + 1], (LANES, LANES)).astype(jnp.int16)
+        return unpack(pairs, k)
 
     def kept(k):
-        return jnp.broadcast_to(wide_ref[:, k : k + 1], (LANES, LANES)).astype(jnp.int16)
+        return unpack(wide_ref[...], k)
 
     def one_hot(column_of):
         rows = []
@@ -297,6 +303,7 @@
         def _():
             pl.semaphore_wait(barrier, heard)
 
+    def pass_on(condition):
         tell(relay_sem.at[0], condition & (z > 0) & (z < ROW - 1), -1)
         tell(relay_sem.at[1], condition & exists(-1) & (z < ROW - 1), 1)
 
@@ -304,6 +311,7 @@
     greet(late)
     send(0, late)
     send(1, crosses)
+    pass_on(late)
 
     spread(middle, 6, window(conv(deposit(MID, FAR, kept), t_high, t_low)))
     near_up[...] = middle[8:16, :] + far[0:8, :]
@@ -319,6 +327,7 @@
     greet(jnp.logical_not(late))
     send(0, jnp.logical_not(late))
     send(2, jnp.logical_not(late))
+    pass_on(jnp.logical_not(late))
 
     def send_down(condition):
         @pl.when(condition & exists(-2) & (z > 0))
@@ -382,7 +391,7 @@
                 pltpu.VMEM((SLOTS, REACH), F32),
                 pltpu.VMEM((WIDE, REACH), BF16),
                 pltpu.VMEM((WIDE, REACH), BF16),
-                pltpu.VMEM((LANES, lines // LANES), jnp.int32),
+                pltpu.VMEM((LANES, lines // LANES // 2), jnp.int32),
                 pltpu.VMEM((3, MID, LANES), F32),
                 pltpu.VMEM((3 * 8, LANES), F32),
                 pltpu.VMEM((2 * 8, LANES), F32),

time: 19.6 us -> 19.5 us (level)
  no operation moved by 1% of the time
where the time goes in v7:
time: 19.5 us; the launch traced here: 19.3 us
  Pallas kernels  18.1 us (93%)
  between operations  0.66 us (3%)
  other arithmetic  0.6 us (3%)
    pallas_call x1, Pallas kernels, body(): pl.pallas_call(call, out_shape=(piece, piece), in_specs=[hbm] * 3 + [pl.B...  18.1 us
    reshape x1, other arithmetic, body(): return (own + received).reshape(SPAN)  0.6 us

profile of v7, /device:TPU:1, one launch (start us, length us, event | category | flops | bytes accessed | tf_op | source)
XLA Modules:
  0.0 19.3 jit_solution(10936641453964842642)
XLA Ops:
  0.7 18.1 %voigt.1 = (f32[8,128]{1,0:T(8,128)S(1)}, f32[8,128]{1,0:T(8,128)S(1)}) custom-call(s32[16,128]{1,0:T(8,128)} %bitcast.8, s32[16,128]{1,0:T(8,128)} %bitcast.9, f32[16,128]{1,0:T(8,128)} %bitcast.10, s32[1]{0:T(128)S(6)} %copy.9.refs_3_, f32[1,32]{1,0:T(1,128)} %bitcast.11, f32[1,32]{1,0:T(1,128)} %bitcast.12, f32[1,32]{1,0:T(1,128)} %bitcast.13, ...), custom_call_target="tpu_custom_call" | custom-call | tf_op jit(solution)/shard_map/voigt/pallas_call | solution.py:378
  18.7 0.6 %add_bitcast_fusion = f32[1024]{0:T(1024)} fusion(f32[8,128]{1,0:T(8,128)S(1)} %get-tuple-element.7, f32[8,128]{1,0:T(8,128)S(1)} %get-tuple-element.8), kind=kLoop, calls=%fused_computation | loop fusion | flops 1024 | bytes 12288 | tf_op jit(solution)/shard_map/reshape | solution.py:426

commit v8 on v7

--- a/solution.py
+++ b/solution.py
@@ -101,6 +101,7 @@
     stage,
     far,
     middle,
+    leak_ref,
     near_up,
     near_down,
     lower,
@@ -180,20 +181,102 @@
     for load in loads[3:]:
         load.wait()
 
+    lane = lax.broadcasted_iota(jnp.int32, (LANES, LANES), 1)
+    spot = lax.broadcasted_iota(jnp.int32, (16, LANES), 0)
+    blocks = lines // LANES
+    zero = jnp.zeros((16, LANES), BF16)
+
+    def tile_of(value, k, dtype):
+        return jnp.broadcast_to(value[k : k + 1, :], (16, LANES)).astype(dtype)
+
+    ahead = n_dev - dev
+    pieces = (far.at[pl.ds(16, 8), :], far.at[pl.ds(8, 8), :], near_up)
+    pieces += (lower.at[pl.ds(0, 16), :], near_down)
+
+    def copy(index, source=None):
+        o = OFFSETS[index]
+        return pltpu.make_async_remote_copy(
+            src_ref=pieces[index] if source is None else source,
+            dst_ref=inbox.at[pl.ds(*SPOTS[index]), :],
+            send_sem=send_sem.at[index],
+            recv_sem=recv_sem.at[index],
+            device_id=(lax.div(me + o, n_dev), lax.rem(me + o, n_dev)),
+            device_id_type=pl.DeviceIdType.MESH,
+        )
+
+    def send(index, condition):
+        o = OFFSETS[index]
+        condition = jnp.logical_and(exists(o), condition)
+
+        @pl.when(condition & (ahead != o) if o > 0 else condition)
+        def _():
+            copy(index).start()
+
+    def leak():
+        within = near - ((n_dev - dev + HOP) * SPAN - LANES)
+        table_high, table_low = split(
+            voigt_table(gauss_ref, lorentz_ref, mixing_ref, factor_ref, padded)
+        )
+        weights_high, weights_low, hits = [], [], []
+        for k in range(blocks):
+            bin_at = tile_of(within, k, jnp.int16)
+            slot_at = tile_of(slot, k, jnp.int16)
+            high = tile_of(weight_high, k, BF16)
+            low = tile_of(weight_low, k, BF16)
+            own = [slot_at == (spot + i * 16).astype(jnp.int16) for i in range(SLOTS // 16)]
+            weights_high.append(jnp.concatenate([jnp.where(hit, high, zero) for hit in own], axis=0))
+            weights_low.append(jnp.concatenate([jnp.where(hit, low, zero) for hit in own], axis=0))
+            hits.append(
+                jnp.concatenate(
+                    [
+                        jnp.where(
+                            bin_at == (spot + i * 16).astype(jnp.int16),
+                            jnp.ones((16, LANES), BF16),
+                            zero,
+                        )
+                        for i in range(LANES // 16)
+                    ],
+                    axis=0,
+                )
+            )
+        hits = jnp.concatenate(hits, axis=1)
+        over_lines = (((1,), (1,)), ((), ()))
+        grid = lax.dot_general(
+            hits, jnp.concatenate(weights_high, axis=1), over_lines, preferred_element_type=F32
+        ) + lax.dot_general(
+            hits, jnp.concatenate(weights_low, axis=1), over_lines, preferred_element_type=F32
+        )
+        high, low = split(grid)
+        kernel_high = table_high[:, 2 * LANES :]
+        kernel_low = table_low[:, 2 * LANES :]
+        spread_out = (
+            jnp.dot(high, kernel_high, preferred_element_type=F32)
+            + jnp.dot(low, kernel_high, preferred_element_type=F32)
+            + jnp.dot(high, kernel_low, preferred_element_type=F32)
+        )
+        moved = pltpu.roll(spread_out, 1, 1, stride=1, stride_axis=0)
+        row = lax.broadcasted_iota(jnp.int32, (LANES, LANES), 0)
+        return jnp.sum(jnp.where(lane <= row, moved, 0.0), axis=0, keepdims=True)
+
+    edge = (ahead <= 3) & (me + ahead < devices)
+
+    @pl.when(edge)
+    def _():
+        leak_ref[...] = jnp.zeros((8, LANES), F32)
+        leak_ref[0:1, :] = leak()
+        pl.semaphore_wait(barrier, heard)
+        for index in range(3):
+
+            @pl.when(ahead == OFFSETS[index])
+            def _():
+                copy(index, leak_ref).start()
+
     table = voigt_table(gauss_ref, lorentz_ref, mixing_ref, factor_ref, padded)
     table_high, table_low = split(table)
     for r in range(PART):
         rows = slice(r * SLOTS, (r + 1) * SLOTS)
         t_high[rows, :] = pltpu.roll(table_high, r + 2 * LANES + 1, 1)
         t_low[rows, :] = pltpu.roll(table_low, r + 2 * LANES + 1, 1)
-
-    lane = lax.broadcasted_iota(jnp.int32, (LANES, LANES), 1)
-    spot = lax.broadcasted_iota(jnp.int32, (16, LANES), 0)
-    blocks = lines // LANES
-    zero = jnp.zeros((16, LANES), BF16)
-
-    def tile_of(value, k, dtype):
-        return jnp.broadcast_to(value[k : k + 1, :], (16, LANES)).astype(dtype)
 
     pairs = wide[:, 0:(blocks // 2)] + wide[:, (blocks // 2) : 2 * (blocks // 2)] * 65536
     wide_ref[...] = pairs
@@ -279,25 +362,6 @@
         target[at + 1 : at + 1 + rows, :] += value[:, LANES : 2 * LANES]
         target[at + 2 : at + 2 + rows, :] += value[:, 2 * LANES : 3 * LANES]
 
-    pieces = (far.at[pl.ds(16, 8), :], far.at[pl.ds(8, 8), :], near_up)
-    pieces += (lower.at[pl.ds(0, 16), :], near_down)
-
-    def copy(index):
-        o = OFFSETS[index]
-        return pltpu.make_async_remote_copy(
-            src_ref=pieces[index],
-            dst_ref=inbox.at[pl.ds(*SPOTS[index]), :],
-            send_sem=send_sem.at[index],
-            recv_sem=recv_sem.at[index],
-            device_id=(lax.div(me + o, n_dev), lax.rem(me + o, n_dev)),
-            device_id_type=pl.DeviceIdType.MESH,
-        )
-
-    def send(index, condition):
-        @pl.when(jnp.logical_and(exists(OFFSETS[index]), condition))
-        def _():
-            copy(index).start()
-
     def greet(condition):
         @pl.when(condition)
         def _():
@@ -308,7 +372,7 @@
         tell(relay_sem.at[1], condition & exists(-1) & (z < ROW - 1), 1)
 
     spread(far, 6, window(conv(deposit(FAR, CELLS, columns), t_high, t_low)))
-    greet(late)
+    greet(late & jnp.logical_not(edge))
     send(0, late)
     send(1, crosses)
     pass_on(late)
@@ -395,6 +459,7 @@
                 pltpu.VMEM((3, MID, LANES), F32),
                 pltpu.VMEM((3 * 8, LANES), F32),
                 pltpu.VMEM((2 * 8, LANES), F32),
+                pltpu.VMEM((8, LANES), F32),
                 pltpu.VMEM((8, LANES), F32),
                 pltpu.VMEM((8, LANES), F32),
                 pltpu.VMEM((4 * 8, LANES), F32),

time: 19.5 us -> 19.2 us (0.985)
  Pallas kernels: 18.1 us -> 17.7 us
    pallas_call x1, Pallas kernels: 18.1 us -> 17.7 us  [body(): pl.pallas_call(call, out_shape=(piece, piece), in_specs=[hbm] * 3 + [pl.B...]
where the time goes in v8:
time: 19.2 us; the launch traced here: 19 us
  Pallas kernels  17.7 us (92%)
  between operations  0.66 us (3%)
  other arithmetic  0.6 us (3%)
    pallas_call x1, Pallas kernels, body(): pl.pallas_call(call, out_shape=(piece, piece), in_specs=[hbm] * 3 + [pl.B...  17.7 us
    reshape x1, other arithmetic, body(): return (own + received).reshape(SPAN)  0.6 us

profile of v8, /device:TPU:1, one launch (start us, length us, event | category | flops | bytes accessed | tf_op | source)
XLA Modules:
  0.0 19.0 jit_solution(11995480388548639591)
XLA Ops:
  0.7 17.7 %voigt.1 = (f32[8,128]{1,0:T(8,128)S(1)}, f32[8,128]{1,0:T(8,128)S(1)}) custom-call(s32[16,128]{1,0:T(8,128)} %bitcast.8, s32[16,128]{1,0:T(8,128)} %bitcast.9, f32[16,128]{1,0:T(8,128)} %bitcast.10, s32[1]{0:T(128)S(6)} %copy.9.refs_3_, f32[1,32]{1,0:T(1,128)} %bitcast.11, f32[1,32]{1,0:T(1,128)} %bitcast.12, f32[1,32]{1,0:T(1,128)} %bitcast.13, ...), custom_call_target="tpu_custom_call" | custom-call | tf_op jit(solution)/shard_map/voigt/pallas_call | solution.py:442
  18.4 0.6 %add_bitcast_fusion = f32[1024]{0:T(1024)} fusion(f32[8,128]{1,0:T(8,128)S(1)} %get-tuple-element.7, f32[8,128]{1,0:T(8,128)S(1)} %get-tuple-element.8), kind=kLoop, calls=%fused_computation | loop fusion | flops 1024 | bytes 12288 | tf_op jit(solution)/shard_map/reshape | solution.py:491
